TPU v7x, 32 devices: a whole 2x2x4 slice. The times are simulated.
32 devices in a mesh: gx: 4 (over z), gy: 4 (over y, x), gz: 2 (over core).
Axes of the slice: x: 2, y: 2, z: 4, core: 2. Of those that a mesh axis runs over, the one named last changes fastest.
Arguments:
- signal: float32 [16, 131072], P(None, ('gx', 'gy', 'gz')), may hold values from -6 to 6
- order: int32 [131072], P(('gx', 'gy', 'gz')), may hold values from 0 to 4095, as said below
- near_tiles: bfloat16 [512, 3, 256, 256], P(('gx', 'gy', 'gz')), may hold values from -0.21875 to 0.21875
- near_list: int32 [512, 3], P(('gx', 'gy', 'gz')), may hold values from 0 to 511, as said below
- leaf_basis: bfloat16 [512, 64, 256], P(('gx', 'gy', 'gz')), may hold values from -0.375 to 0.375
- leaf_transfer: bfloat16 [512, 64, 64], P(('gx', 'gy', 'gz')), may hold values from -0.5 to 0.5
- leaf_coupling: bfloat16 [512, 64, 192], P(('gx', 'gy', 'gz')), may hold values from -0.4375 to 0.4375
- leaf_links: int32 [512, 3], P(('gx', 'gy', 'gz')), may hold values from 0 to 511, as said below
- device_transfer: bfloat16 [32, 64, 64], P(('gx', 'gy', 'gz')), may hold values from -0.5 to 0.5
- device_coupling: bfloat16 [32, 64, 192], P(('gx', 'gy', 'gz')), may hold values from -0.15625 to 0.15625
- device_links: int32 [32, 3], P(('gx', 'gy', 'gz')), may hold values from 0 to 31, as said below
- block_transfer: bfloat16 [16, 64, 64], P(('gx', 'gy')), may hold values from -0.5 to 0.5
- block_coupling: bfloat16 [16, 64, 192], P(('gx', 'gy')), may hold values from -0.15625 to 0.15625
- block_links: int32 [16, 3], P(('gx', 'gy')), may hold values from 0 to 15, as said below
- top_coupling: bfloat16 [4, 64, 192], P('gx'), may hold values from -0.109375 to 0.109375
- top_links: int32 [4, 3], P('gx'), may hold values from 0 to 3, as said below
Outputs:
- smoothed: float32 [16, 131072], P(None, ('gx', 'gy', 'gz'))
- twice: float32 [16, 131072], P(None, ('gx', 'gy', 'gz'))
Inputs may be any that keep to these rules, and one draw needn't show every extreme that they name: `order`: each device's block of 4096 consecutive entries is a permutation of 0 to 4095. `near_list`: row i holds i first, then two different leaves j with 1 <= |j - i| <= 2. `leaf_links`: row i holds three different leaves j with 2 <= |j - i| <= 4. `device_links`: row i holds three different device clusters j with 1 <= |j - i| <= 3. `block_links`: row i holds three different second-level clusters other than i. `top_links`: row i holds three different first-level clusters other than i.
All inputs are finite; a program needn't handle non-finite values.
Results may differ from a plain program's by a relative error of at most 0.0043.
Values may be sent and summed in bfloat16 or wider, within the bound.
No kernel may reach another device: no remote copies, remote signals or barrier semaphores. Data moves between devices by JAX's collectives and lax.ppermute only.
A program may use at most 64 MiB of HBM per device.

v0:
```python
import jax
import jax.numpy as jnp
from jax import lax
from jax.sharding import PartitionSpec as P

NEAR_REACH = 2
LINK_REACH = 4
DEVICE_REACH = 3


HIGH = lax.Precision.HIGHEST


def shifted(block, axis, distance):
    devices = range(lax.axis_size(axis))
    route = [(i - distance, i) for i in devices if i - distance in devices]
    return lax.ppermute(block, axis, route)


def couple(picked, coupling):
    rank_dim = coupling.shape[0]
    link_count = picked.shape[0]
    table = coupling.astype(jnp.float32).reshape(rank_dim, link_count, rank_dim)
    return jnp.einsum("jrk,kjm->rm", picked, table, precision=HIGH)


def spread_down(parent, transfer):
    return jnp.dot(parent, transfer.astype(jnp.float32).T, precision=HIGH)


def relay_side(own_moment, direction):
    window = own_moment[None][:0]
    for step in range(DEVICE_REACH):
        outgoing = jnp.concatenate([own_moment[None], window], axis=0)
        window = shifted(outgoing, ("gx", "gy", "gz"), direction)
    return window


def apply_matrix(
    leaves,
    near_tiles,
    near_list,
    leaf_basis,
    leaf_transfer,
    leaf_coupling,
    leaf_links,
    device_transfer,
    device_coupling,
    device_links,
    block_transfer,
    block_coupling,
    block_links,
    top_coupling,
    top_links,
):
    leaf_dev = leaves.shape[1]
    device = lax.axis_index(("gx", "gy", "gz"))
    first_leaf = device * leaf_dev
    rims = []
    for offset, edge in ((1, leaves[:, leaf_dev - NEAR_REACH :]), (-1, leaves[:, :NEAR_REACH])):
        rims.append(shifted(edge, ("gx", "gy", "gz"), offset))
    widened = jnp.concatenate([rims[0], leaves, rims[1]], axis=1)
    moments = jnp.einsum("rls,lks->rlk", leaves, leaf_basis, preferred_element_type=jnp.float32)
    edges = []
    for offset, edge in ((1, moments[:, leaf_dev - LINK_REACH :]), (-1, moments[:, :LINK_REACH])):
        edges.append(shifted(edge, ("gx", "gy", "gz"), offset))
    wide_moments = jnp.concatenate([edges[0], moments, edges[1]], axis=1)
    transfer_f = leaf_transfer.astype(jnp.float32)
    own_moment = jnp.einsum("rlk,lkm->rm", moments, transfer_f, precision=HIGH)
    block_term = jnp.dot(own_moment, device_transfer[0].astype(jnp.float32), precision=HIGH)
    block_moment = lax.psum(block_term, "gz")
    lower = relay_side(own_moment, 1)
    upper = relay_side(own_moment, -1)
    stacked = jnp.concatenate([lower[::-1], upper], axis=0)
    relative = device_links[0] - device
    position = relative + DEVICE_REACH - (relative > 0).astype(jnp.int32)
    device_picked = stacked[position]
    top_term = jnp.dot(block_moment, block_transfer[0].astype(jnp.float32), precision=HIGH)
    top_moment = lax.psum(top_term, "gy")
    every_top = lax.all_gather(top_moment[None], "gx", axis=0, tiled=True)
    every_block = lax.all_gather(block_moment[None], ("gx", "gy"), axis=0, tiled=True)
    top_field = couple(every_top[top_links[0]], top_coupling[0])
    block_field = couple(every_block[block_links[0]], block_coupling[0]) + spread_down(
        top_field, block_transfer[0]
    )
    device_field = couple(device_picked, device_coupling[0]) + spread_down(
        block_field, device_transfer[0]
    )
    local_links = leaf_links - first_leaf + LINK_REACH
    picked = wide_moments[:, local_links]
    rank_dim = leaf_coupling.shape[1]
    leaf_table = leaf_coupling.astype(jnp.float32).reshape(leaf_dev, rank_dim, -1, rank_dim)
    leaf_field = jnp.einsum("rljk,lkjm->rlm", picked, leaf_table, precision=HIGH)
    leaf_field = leaf_field + jnp.einsum("rm,lkm->rlk", device_field, transfer_f, precision=HIGH)
    far_part = jnp.einsum(
        "rlk,lks->rls",
        leaf_field.astype(jnp.bfloat16),
        leaf_basis,
        preferred_element_type=jnp.float32,
    )
    near_index = near_list - first_leaf + NEAR_REACH
    near_rows = widened[:, near_index]
    near_part = jnp.einsum(
        "rlns,lnst->rlt", near_rows, near_tiles, preferred_element_type=jnp.float32
    )
    return near_part + far_part


def shards(
    signal,
    order,
    near_tiles,
    near_list,
    leaf_basis,
    leaf_transfer,
    leaf_coupling,
    leaf_links,
    device_transfer,
    device_coupling,
    device_links,
    block_transfer,
    block_coupling,
    block_links,
    top_coupling,
    top_links,
):
    matrices = (
        near_tiles,
        near_list,
        leaf_basis,
        leaf_transfer,
        leaf_coupling,
        leaf_links,
        device_transfer,
        device_coupling,
        device_links,
        block_transfer,
        block_coupling,
        block_links,
        top_coupling,
        top_links,
    )
    rhs_count = signal.shape[0]
    leaf_count = near_tiles.shape[0]
    tree = jnp.take(signal, order, axis=1).astype(jnp.bfloat16).reshape(rhs_count, leaf_count, -1)
    first = apply_matrix(tree, *matrices)
    second = apply_matrix(first.astype(jnp.bfloat16), *matrices)
    empty = jnp.zeros_like(signal)
    smoothed = empty.at[:, order].set(first.reshape(rhs_count, -1))
    twice = empty.at[:, order].set(second.reshape(rhs_count, -1))
    return (smoothed, twice)


def solution(mesh):
    in_specs = (
        P(None, ("gx", "gy", "gz")),
        P(("gx", "gy", "gz")),
        P(("gx", "gy", "gz"), None, None, None),
        P(("gx", "gy", "gz"), None),
        P(("gx", "gy", "gz"), None, None),
        P(("gx", "gy", "gz"), None, None),
        P(("gx", "gy", "gz"), None, None),
        P(("gx", "gy", "gz"), None),
        P(("gx", "gy", "gz"), None, None),
        P(("gx", "gy", "gz"), None, None),
        P(("gx", "gy", "gz"), None),
        P(("gx", "gy"), None, None),
        P(("gx", "gy"), None, None),
        P(("gx", "gy"), None),
        P("gx", None, None),
        P("gx", None),
    )
    out_specs = (P(None, ("gx", "gy", "gz")), P(None, ("gx", "gy", "gz")))
    return jax.shard_map(shards, mesh=mesh, in_specs=in_specs, out_specs=out_specs, check_vma=False)
```

profile of v0, /device:TPU:1, one launch (start us, length us, event | category | flops | bytes accessed | tf_op | source)
XLA Modules:
  0.0 251.4 jit_solution(4829175544819906488)
XLA Ops:
  4.4 12.1 %gather_fusion = bf16[4096,16]{1,0:T(8,128)(2,1)S(1)} fusion(bf16[16,4096]{0,1:T(8,128)(2,1)S(1)} %copy.38, s32[4096]{0:T(1024)S(1)} %get-tuple-element.16), kind=kCustom, calls=%fused_computation | custom fusion | bytes 278528 | tf_op jit(solution)/shard_map/jit(_take)/gather | solution.py:145
  17.4 1.9 collective-permute-start.7
  19.4 4.5 %collective-permute-start.4 = (f32[1,16,64]{2,1,0:T(8,128)S(1)}, f32[1,16,64]{2,1,0:T(8,128)S(1)}, u32[]{:S(2)}, u32[]{:S(2)}) collective-permute-start(f32[1,16,64]{2,1,0:T(8,128)S(1)} %bitcast.194), channel_id=1, source_target_pairs={{0,1},{1,2},{2,3},{3,4},{4,5},{5,6},{6,7},{7,8},{8,9},{9,10},{10,1... | collective-permute-start | bytes 12296 | tf_op jit(solution)/shard_map/ppermute | solution.py:17
  23.9 2.4 collective-permute-start
  26.3 1.9 collective-permute-start.1
  28.2 3.9 %collective-permute-start.2 = (f32[16,4,64]{2,0,1:T(8,128)S(1)}, f32[16,4,64]{2,0,1:T(8,128)S(1)}, u32[]{:S(2)}, u32[]{:S(2)}) collective-permute-start(f32[16,4,64]{2,0,1:T(8,128)S(1)} %get-tuple-element.12), channel_id=1, source_target_pairs={{0,1},{1,2},{2,3},{3,4},{4,5},{5,6},{6,7},{7,8},{8,9},{9,10},{10,1... | collective-permute-start | bytes 49160 | tf_op jit(solution)/shard_map/ppermute | solution.py:17
  32.8 2.5 psum.28
  35.3 32.7 %all-gather = f32[256,64]{1,0:T(8,128)S(1)} all-gather(f32[16,64]{1,0:T(8,128)S(1)} %psum.28), channel_id=2, replica_groups=mesh['gx'=4,'gy'=4,'gz'=2] {'gx','gy'}, dimensions={0}, use_global_device_ids=true | all-gather | bytes 69632 | tf_op jit(solution)/shard_map/all_gather | solution.py:81
  68.2 6.2 %psum.29 = f32[1,16,64]{2,1,0:T(8,128)S(1)} all-reduce(f32[1,16,64]{2,1,0:T(8,128)S(1)} %convolution_bitcast_fusion.11), channel_id=1, replica_groups=mesh['gx'=4,'gy'=4,'gz'=2] {'gy'}, use_global_device_ids=true, to_apply=%region_1.2 | all-reduce | flops 1024 | bytes 8192 | tf_op jit(solution)/shard_map/psum | solution.py:79
  74.3 10.3 %all_gather.13 = f32[4,16,64]{2,1,0:T(8,128)S(1)} all-gather(f32[1,16,64]{2,1,0:T(8,128)S(1)} %psum.29), channel_id=1, replica_groups=mesh['gx'=4,'gy'=4,'gz'=2] {'gx'}, dimensions={0}, use_global_device_ids=true | all-gather | bytes 20480 | tf_op jit(solution)/shard_map/all_gather | solution.py:80
  86.6 15.3 %collective-permute-start.5 = (f32[2,16,64]{2,1,0:T(8,128)S(1)}, f32[2,16,64]{2,1,0:T(8,128)S(1)}, u32[]{:S(2)}, u32[]{:S(2)}) collective-permute-start(f32[2,16,64]{2,1,0:T(8,128)S(1)} %get-tuple-element.24), channel_id=1, source_target_pairs={{0,1},{1,2},{2,3},{3,4},{4,5},{5,6},{6,7},{7,8},{8,9},{9,10},{10,1... | collective-permute-start | bytes 24584 | tf_op jit(solution)/shard_map/ppermute | solution.py:17
  101.9 1.9 collective-permute-start.8
  107.0 3.0 %collective-permute-start.6 = (f32[3,16,64]{2,1,0:T(8,128)S(1)}, f32[3,16,64]{2,1,0:T(8,128)S(1)}, u32[]{:S(2)}, u32[]{:S(2)}) collective-permute-start(f32[3,16,64]{2,1,0:T(8,128)S(1)} %get-tuple-element.22), channel_id=1, source_target_pairs={{0,1},{1,2},{2,3},{3,4},{4,5},{5,6},{6,7},{7,8},{8,9},{9,10},{10,1... | collective-permute-start | bytes 36872 | tf_op jit(solution)/shard_map/ppermute | solution.py:17
  110.0 1.9 collective-permute-start.9
  112.6 3.7 %convolution_bitcast_fusion.1 = f32[16,16,256]{2,1,0:T(8,128)S(1)} fusion(bf16[16,16,3,256]{3,0,2,1:T(8,128)(2,1)S(1)} %bitcast.178, bf16[16,3,256,256]{3,2,1,0:T(8,128)(2,1)} %param.18), kind=kOutput, calls=%fused_computation.17 | convolution fusion | flops 100663296 | bytes 6946816 | tf_op jit(solution)/shard_map/rlns,lnst->rlt/dot_general | solution.py:103
  120.9 1.9 collective-permute-start.17
  122.9 3.6 %collective-permute-start.14 = (f32[1,16,64]{2,1,0:T(8,128)S(1)}, f32[1,16,64]{2,1,0:T(8,128)S(1)}, u32[]{:S(2)}, u32[]{:S(2)}) collective-permute-start(f32[1,16,64]{2,1,0:T(8,128)S(1)} %bitcast.198), channel_id=1, source_target_pairs={{0,1},{1,2},{2,3},{3,4},{4,5},{5,6},{6,7},{7,8},{8,9},{9,10},{10,1... | collective-permute-start | bytes 12296 | tf_op jit(solution)/shard_map/ppermute | solution.py:17
  127.1 2.5 psum.30
  129.7 31.1 %all-gather.1 = f32[256,64]{1,0:T(8,128)S(1)} all-gather(f32[16,64]{1,0:T(8,128)S(1)} %psum.30), channel_id=3, replica_groups=mesh['gx'=4,'gy'=4,'gz'=2] {'gx','gy'}, dimensions={0}, use_global_device_ids=true | all-gather | bytes 69632 | tf_op jit(solution)/shard_map/all_gather | solution.py:81
  160.8 8.7 %collective-permute-start.10 = (bf16[16,2,256]{2,0,1:T(8,128)(2,1)}, bf16[16,2,256]{2,0,1:T(8,128)(2,1)}, u32[]{:S(2)}, u32[]{:S(2)}) collective-permute-start(bf16[16,2,256]{2,0,1:T(8,128)(2,1)} %get-tuple-element.10), channel_id=1, source_target_pairs={{0,1},{1,2},{2,3},{3,4},{4,5},{5,6},{6,7},{7,8},{8,9},{9,10},{10,1... | collective-permute-start | bytes 49160 | tf_op jit(solution)/shard_map/ppermute | solution.py:17
  169.6 2.4 collective-permute-start.11
  172.0 5.9 %psum.31 = f32[1,16,64]{2,1,0:T(8,128)S(1)} all-reduce(f32[1,16,64]{2,1,0:T(8,128)S(1)} %convolution_bitcast_fusion.7), channel_id=1, replica_groups=mesh['gx'=4,'gy'=4,'gz'=2] {'gy'}, use_global_device_ids=true, to_apply=%region_4.5 | all-reduce | flops 1024 | bytes 8192 | tf_op jit(solution)/shard_map/psum | solution.py:79
  177.9 10.4 %all_gather.15 = f32[4,16,64]{2,1,0:T(8,128)S(1)} all-gather(f32[1,16,64]{2,1,0:T(8,128)S(1)} %psum.31), channel_id=1, replica_groups=mesh['gx'=4,'gy'=4,'gz'=2] {'gx'}, dimensions={0}, use_global_device_ids=true | all-gather | bytes 20480 | tf_op jit(solution)/shard_map/all_gather | solution.py:80
  189.0 7.3 %collective-permute-start.12 = (f32[16,4,64]{2,0,1:T(8,128)}, f32[16,4,64]{2,0,1:T(8,128)}, u32[]{:S(2)}, u32[]{:S(2)}) collective-permute-start(f32[16,4,64]{2,0,1:T(8,128)} %get-tuple-element.8), channel_id=1, source_target_pairs={{0,1},{1,2},{2,3},{3,4},{4,5},{5,6},{6,7},{7,8},{8,9},{9,10},{10,1... | collective-permute-start | bytes 49160 | tf_op jit(solution)/shard_map/ppermute | solution.py:17
  199.8 3.0 %collective-permute-start.18 = (f32[2,16,64]{2,1,0:T(8,128)}, f32[2,16,64]{2,1,0:T(8,128)}, u32[]{:S(2)}, u32[]{:S(2)}) collective-permute-start(f32[2,16,64]{2,1,0:T(8,128)} %get-tuple-element.21), channel_id=1, source_target_pairs={{1,0},{2,1},{3,2},{4,3},{5,4},{6,5},{7,6},{8,7},{9,8},{10,9},{11,1... | collective-permute-start | bytes 24584 | tf_op jit(solution)/shard_map/ppermute | solution.py:17
  203.6 2.0 copy.51
  205.6 11.4 %scatter_custom_fusion = f32[16,4096]{0,1:T(8,128)S(1)} fusion(s32[4096]{0:T(1024)} %get-tuple-element.17, f32[4096,16]{1,0:T(8,128)} %copy.51, f32[]{:T(128)} %constant.15.clone.1), kind=kCustom, calls=%fused_computation.42 | custom fusion | bytes 262656 | tf_op jit(solution)/shard_map/scatter | solution.py:149
  220.9 4.1 %collective-permute-start.16 = (f32[3,16,64]{2,1,0:T(8,128)S(1)}, f32[3,16,64]{2,1,0:T(8,128)S(1)}, u32[]{:S(2)}, u32[]{:S(2)}) collective-permute-start(f32[3,16,64]{2,1,0:T(8,128)S(1)} %get-tuple-element.18), channel_id=1, source_target_pairs={{0,1},{1,2},{2,3},{3,4},{4,5},{5,6},{6,7},{7,8},{8,9},{9,10},{10,1... | collective-permute-start | bytes 36872 | tf_op jit(solution)/shard_map/ppermute | solution.py:17
  225.1 2.1 collective-permute-start.19
  228.8 3.8 %convolution_bitcast_fusion = f32[16,16,256]{2,1,0:T(8,128)S(1)} fusion(bf16[16,16,3,256]{3,0,2,1:T(8,128)(2,1)S(1)} %bitcast.177, bf16[16,3,256,256]{3,2,1,0:T(8,128)(2,1)} %param.18), kind=kOutput, calls=%fused_computation.15 | convolution fusion | flops 100663296 | bytes 6946816 | tf_op jit(solution)/shard_map/rlns,lnst->rlt/dot_general | solution.py:103
  236.8 2.0 copy.57
  238.7 11.4 %scatter_custom_fusion.1 = f32[16,4096]{0,1:T(8,128)S(1)} fusion(s32[4096]{0:T(1024)} %get-tuple-element.17, f32[4096,16]{1,0:T(8,128)} %copy.57, f32[]{:T(128)} %constant.15.clone.1), kind=kCustom, calls=%fused_computation.40 | custom fusion | bytes 262656 | tf_op jit(solution)/shard_map/scatter | solution.py:150
  (152 shorter events, 31.8 us)
Async XLA Ops:
  4.3 28.0 %copy-start.21 = (s32[16,3]{0,1:T(4,128)S(1)}, s32[16,3]{0,1:T(4,128)}, u32[]{:S(2)}) copy-start(s32[16,3]{0,1:T(4,128)} %param.23) | copy-start | bytes 580
  4.3 27.9 %copy-start.22 = (s32[16,3]{0,1:T(4,128)S(1)}, s32[16,3]{0,1:T(4,128)}, u32[]{:S(2)}) copy-start(s32[16,3]{0,1:T(4,128)} %param.19) | copy-start | bytes 580
  4.3 28.1 %copy-start.16 = (bf16[1,64,192]{2,1,0:T(8,128)(2,1)S(1)}, bf16[1,64,192]{2,1,0:T(8,128)(2,1)}, u32[]{:S(2)}) copy-start(bf16[1,64,192]{2,1,0:T(8,128)(2,1)} %param.28) | copy-start | bytes 73732
  4.3 28.3 %copy-start.17 = (bf16[1,64,192]{2,1,0:T(8,128)(2,1)S(1)}, bf16[1,64,192]{2,1,0:T(8,128)(2,1)}, u32[]{:S(2)}) copy-start(bf16[1,64,192]{2,1,0:T(8,128)(2,1)} %param.30) | copy-start | bytes 73732
  4.3 28.4 %copy-start.8 = (bf16[1,64,64]{2,1,0:T(8,128)(2,1)S(1)}, bf16[1,64,64]{2,1,0:T(8,128)(2,1)}, u32[]{:S(2)}) copy-start(bf16[1,64,64]{2,1,0:T(8,128)(2,1)} %param.24) | copy-start | bytes 24580
  4.3 63.7 %copy-start.7 = (bf16[1,64,64]{2,1,0:T(8,128)(2,1)S(1)}, bf16[1,64,64]{2,1,0:T(8,128)(2,1)}, u32[]{:S(2)}) copy-start(bf16[1,64,64]{2,1,0:T(8,128)(2,1)} %param.27) | copy-start | bytes 24580
  16.5 87.4 %copy-start.18 = (bf16[1,64,192]{2,1,0:T(8,128)(2,1)S(1)}, bf16[1,64,192]{2,1,0:T(8,128)(2,1)}, u32[]{:S(2)}) copy-start(bf16[1,64,192]{2,1,0:T(8,128)(2,1)} %param.25) | copy-start | bytes 73732
  16.5 87.5 %copy-start.4 = (bf16[16,64,192]{2,1,0:T(8,128)(2,1)S(1)}, bf16[16,64,192]{2,1,0:T(8,128)(2,1)}, u32[]{:S(2)}) copy-start(bf16[16,64,192]{2,1,0:T(8,128)(2,1)} %param.22) | copy-start | bytes 1179652
  17.4 69.1 %collective-permute-start.7 = (f32[1,16,64]{2,1,0:T(8,128)S(1)}, f32[1,16,64]{2,1,0:T(8,128)S(1)}, u32[]{:S(2)}, u32[]{:S(2)}) collective-permute-start(f32[1,16,64]{2,1,0:T(8,128)S(1)} %bitcast.193), channel_id=1, source_target_pairs={{1,0},{2,1},{3,2},{4,3},{5,4},{6,5},{7,6},{8,7},{9,8},{10,9},{11,1... | collective-permute-start | bytes 12296 | tf_op jit(solution)/shard_map/ppermute | solution.py:17
  19.4 67.2 %collective-permute-start.4 = (f32[1,16,64]{2,1,0:T(8,128)S(1)}, f32[1,16,64]{2,1,0:T(8,128)S(1)}, u32[]{:S(2)}, u32[]{:S(2)}) collective-permute-start(f32[1,16,64]{2,1,0:T(8,128)S(1)} %bitcast.194), channel_id=1, source_target_pairs={{0,1},{1,2},{2,3},{3,4},{4,5},{5,6},{6,7},{7,8},{8,9},{9,10},{10,1... | collective-permute-start | bytes 12296 | tf_op jit(solution)/shard_map/ppermute | solution.py:17
  23.9 86.1 %collective-permute-start = (bf16[16,2,256]{2,0,1:T(8,128)(2,1)S(1)}, bf16[16,2,256]{2,0,1:T(8,128)(2,1)S(1)}, u32[]{:S(2)}, u32[]{:S(2)}) collective-permute-start(bf16[16,2,256]{2,0,1:T(8,128)(2,1)S(1)} %get-tuple-element.14), channel_id=1, source_target_pairs={{0,1},{1,2},{2,3},{3,4},{4,5},{5,6},{6,7},{7,8},{8,9},{9,10},{10,1... | collective-permute-start | bytes 49160 | tf_op jit(solution)/shard_map/ppermute | solution.py:17
  26.3 85.7 %collective-permute-start.1 = (bf16[16,2,256]{2,0,1:T(8,128)(2,1)S(1)}, bf16[16,2,256]{2,0,1:T(8,128)(2,1)S(1)}, u32[]{:S(2)}, u32[]{:S(2)}) collective-permute-start(bf16[16,2,256]{2,0,1:T(8,128)(2,1)S(1)} %get-tuple-element.15), channel_id=1, source_target_pairs={{1,0},{2,1},{3,2},{4,3},{5,4},{6,5},{7,6},{8,7},{9,8},{10,9},{11,1... | collective-permute-start | bytes 49160 | tf_op jit(solution)/shard_map/ppermute | solution.py:17
  28.2 88.1 %collective-permute-start.2 = (f32[16,4,64]{2,0,1:T(8,128)S(1)}, f32[16,4,64]{2,0,1:T(8,128)S(1)}, u32[]{:S(2)}, u32[]{:S(2)}) collective-permute-start(f32[16,4,64]{2,0,1:T(8,128)S(1)} %get-tuple-element.12), channel_id=1, source_target_pairs={{0,1},{1,2},{2,3},{3,4},{4,5},{5,6},{6,7},{7,8},{8,9},{9,10},{10,1... | collective-permute-start | bytes 49160 | tf_op jit(solution)/shard_map/ppermute | solution.py:17
  32.3 84.8 %copy-start.20 = (s32[1024]{0:T(1024)}, s32[1024]{0:T(1024)S(1)}, u32[]{:S(2)}) copy-start(s32[1024]{0:T(1024)S(1)} %pad_clamp_fusion.2) | copy-start | bytes 12292
  86.4 30.0 %copy-start.12 = (s32[1024]{0:T(1024)}, s32[1024]{0:T(1024)S(1)}, u32[]{:S(2)}) copy-start(s32[1024]{0:T(1024)S(1)} %pad_clamp_fusion.3) | copy-start | bytes 12292
  86.6 17.8 %collective-permute-start.5 = (f32[2,16,64]{2,1,0:T(8,128)S(1)}, f32[2,16,64]{2,1,0:T(8,128)S(1)}, u32[]{:S(2)}, u32[]{:S(2)}) collective-permute-start(f32[2,16,64]{2,1,0:T(8,128)S(1)} %get-tuple-element.24), channel_id=1, source_target_pairs={{0,1},{1,2},{2,3},{3,4},{4,5},{5,6},{6,7},{7,8},{8,9},{9,10},{10,1... | collective-permute-start | bytes 24584 | tf_op jit(solution)/shard_map/ppermute | solution.py:17
  101.9 5.1 %collective-permute-start.8 = (f32[2,16,64]{2,1,0:T(8,128)S(1)}, f32[2,16,64]{2,1,0:T(8,128)S(1)}, u32[]{:S(2)}, u32[]{:S(2)}) collective-permute-start(f32[2,16,64]{2,1,0:T(8,128)S(1)} %get-tuple-element.25), channel_id=1, source_target_pairs={{1,0},{2,1},{3,2},{4,3},{5,4},{6,5},{7,6},{8,7},{9,8},{10,9},{11,1... | collective-permute-start | bytes 24584 | tf_op jit(solution)/shard_map/ppermute | solution.py:17
  104.4 11.9 %collective-permute-start.3 = (f32[16,4,64]{2,0,1:T(8,128)S(1)}, f32[16,4,64]{2,0,1:T(8,128)S(1)}, u32[]{:S(2)}, u32[]{:S(2)}) collective-permute-start(f32[16,4,64]{2,0,1:T(8,128)S(1)} %get-tuple-element.13), channel_id=1, source_target_pairs={{1,0},{2,1},{3,2},{4,3},{5,4},{6,5},{7,6},{8,7},{9,8},{10,9},{11,1... | collective-permute-start | bytes 49160 | tf_op jit(solution)/shard_map/ppermute | solution.py:17
  107.0 10.0 %collective-permute-start.6 = (f32[3,16,64]{2,1,0:T(8,128)S(1)}, f32[3,16,64]{2,1,0:T(8,128)S(1)}, u32[]{:S(2)}, u32[]{:S(2)}) collective-permute-start(f32[3,16,64]{2,1,0:T(8,128)S(1)} %get-tuple-element.22), channel_id=1, source_target_pairs={{0,1},{1,2},{2,3},{3,4},{4,5},{5,6},{6,7},{7,8},{8,9},{9,10},{10,1... | collective-permute-start | bytes 36872 | tf_op jit(solution)/shard_map/ppermute | solution.py:17
  110.0 7.0 %collective-permute-start.9 = (f32[3,16,64]{2,1,0:T(8,128)S(1)}, f32[3,16,64]{2,1,0:T(8,128)S(1)}, u32[]{:S(2)}, u32[]{:S(2)}) collective-permute-start(f32[3,16,64]{2,1,0:T(8,128)S(1)} %get-tuple-element.23), channel_id=1, source_target_pairs={{1,0},{2,1},{3,2},{4,3},{5,4},{6,5},{7,6},{8,7},{9,8},{10,9},{11,1... | collective-permute-start | bytes 36872 | tf_op jit(solution)/shard_map/ppermute | solution.py:17
  119.6 85.9 %copy-start.3 = (bf16[16,16,256]{2,0,1:T(8,128)(2,1)}, bf16[16,16,256]{2,0,1:T(8,128)(2,1)S(1)}, u32[]{:S(2)}) copy-start(bf16[16,16,256]{2,0,1:T(8,128)(2,1)S(1)} %get-tuple-element.26) | copy-start | bytes 393220
  120.8 82.8 %copy-start.10 = (f32[16,64,1]{1,0,2:T(8,128)}, f32[16,64,1]{1,0,2:T(8,128)S(1)}, u32[]{:S(2)}) copy-start(f32[16,64,1]{1,0,2:T(8,128)S(1)} %fusion.38) | copy-start | bytes 12292
  120.9 76.3 %collective-permute-start.17 = (f32[1,16,64]{2,1,0:T(8,128)S(1)}, f32[1,16,64]{2,1,0:T(8,128)S(1)}, u32[]{:S(2)}, u32[]{:S(2)}) collective-permute-start(f32[1,16,64]{2,1,0:T(8,128)S(1)} %bitcast.197), channel_id=1, source_target_pairs={{1,0},{2,1},{3,2},{4,3},{5,4},{6,5},{7,6},{8,7},{9,8},{10,9},{11,1... | collective-permute-start | bytes 12296 | tf_op jit(solution)/shard_map/ppermute | solution.py:17
  122.9 74.4 %collective-permute-start.14 = (f32[1,16,64]{2,1,0:T(8,128)S(1)}, f32[1,16,64]{2,1,0:T(8,128)S(1)}, u32[]{:S(2)}, u32[]{:S(2)}) collective-permute-start(f32[1,16,64]{2,1,0:T(8,128)S(1)} %bitcast.198), channel_id=1, source_target_pairs={{0,1},{1,2},{2,3},{3,4},{4,5},{5,6},{6,7},{7,8},{8,9},{9,10},{10,1... | collective-permute-start | bytes 12296 | tf_op jit(solution)/shard_map/ppermute | solution.py:17
  160.8 64.3 %collective-permute-start.10 = (bf16[16,2,256]{2,0,1:T(8,128)(2,1)}, bf16[16,2,256]{2,0,1:T(8,128)(2,1)}, u32[]{:S(2)}, u32[]{:S(2)}) collective-permute-start(bf16[16,2,256]{2,0,1:T(8,128)(2,1)} %get-tuple-element.10), channel_id=1, source_target_pairs={{0,1},{1,2},{2,3},{3,4},{4,5},{5,6},{6,7},{7,8},{8,9},{9,10},{10,1... | collective-permute-start | bytes 49160 | tf_op jit(solution)/shard_map/ppermute | solution.py:17
  169.6 57.6 %collective-permute-start.11 = (bf16[16,2,256]{2,0,1:T(8,128)(2,1)}, bf16[16,2,256]{2,0,1:T(8,128)(2,1)}, u32[]{:S(2)}, u32[]{:S(2)}) collective-permute-start(bf16[16,2,256]{2,0,1:T(8,128)(2,1)} %get-tuple-element.11), channel_id=1, source_target_pairs={{1,0},{2,1},{3,2},{4,3},{5,4},{6,5},{7,6},{8,7},{9,8},{10,9},{11,1... | collective-permute-start | bytes 49160 | tf_op jit(solution)/shard_map/ppermute | solution.py:17
  189.0 43.5 %collective-permute-start.12 = (f32[16,4,64]{2,0,1:T(8,128)}, f32[16,4,64]{2,0,1:T(8,128)}, u32[]{:S(2)}, u32[]{:S(2)}) collective-permute-start(f32[16,4,64]{2,0,1:T(8,128)} %get-tuple-element.8), channel_id=1, source_target_pairs={{0,1},{1,2},{2,3},{3,4},{4,5},{5,6},{6,7},{7,8},{8,9},{9,10},{10,1... | collective-permute-start | bytes 49160 | tf_op jit(solution)/shard_map/ppermute | solution.py:17
  197.9 20.3 %collective-permute-start.15 = (f32[2,16,64]{2,1,0:T(8,128)}, f32[2,16,64]{2,1,0:T(8,128)}, u32[]{:S(2)}, u32[]{:S(2)}) collective-permute-start(f32[2,16,64]{2,1,0:T(8,128)} %get-tuple-element.20), channel_id=1, source_target_pairs={{0,1},{1,2},{2,3},{3,4},{4,5},{5,6},{6,7},{7,8},{8,9},{9,10},{10,1... | collective-permute-start | bytes 24584 | tf_op jit(solution)/shard_map/ppermute | solution.py:17
  199.8 20.4 %collective-permute-start.18 = (f32[2,16,64]{2,1,0:T(8,128)}, f32[2,16,64]{2,1,0:T(8,128)}, u32[]{:S(2)}, u32[]{:S(2)}) collective-permute-start(f32[2,16,64]{2,1,0:T(8,128)} %get-tuple-element.21), channel_id=1, source_target_pairs={{1,0},{2,1},{3,2},{4,3},{5,4},{6,5},{7,6},{8,7},{9,8},{10,9},{11,1... | collective-permute-start | bytes 24584 | tf_op jit(solution)/shard_map/ppermute | solution.py:17
  218.3 14.3 %collective-permute-start.13 = (f32[16,4,64]{2,0,1:T(8,128)}, f32[16,4,64]{2,0,1:T(8,128)S(1)}, u32[]{:S(2)}, u32[]{:S(2)}) collective-permute-start(f32[16,4,64]{2,0,1:T(8,128)} %get-tuple-element.9), channel_id=1, source_target_pairs={{1,0},{2,1},{3,2},{4,3},{5,4},{6,5},{7,6},{8,7},{9,8},{10,9},{11,1... | collective-permute-start | bytes 49160 | tf_op jit(solution)/shard_map/ppermute | solution.py:17
  220.9 13.0 %collective-permute-start.16 = (f32[3,16,64]{2,1,0:T(8,128)S(1)}, f32[3,16,64]{2,1,0:T(8,128)S(1)}, u32[]{:S(2)}, u32[]{:S(2)}) collective-permute-start(f32[3,16,64]{2,1,0:T(8,128)S(1)} %get-tuple-element.18), channel_id=1, source_target_pairs={{0,1},{1,2},{2,3},{3,4},{4,5},{5,6},{6,7},{7,8},{8,9},{9,10},{10,1... | collective-permute-start | bytes 36872 | tf_op jit(solution)/shard_map/ppermute | solution.py:17
  225.1 8.9 %collective-permute-start.19 = (f32[3,16,64]{2,1,0:T(8,128)S(1)}, f32[3,16,64]{2,1,0:T(8,128)S(1)}, u32[]{:S(2)}, u32[]{:S(2)}) collective-permute-start(f32[3,16,64]{2,1,0:T(8,128)S(1)} %get-tuple-element.19), channel_id=1, source_target_pairs={{1,0},{2,1},{3,2},{4,3},{5,4},{6,5},{7,6},{8,7},{9,8},{10,9},{11,1... | collective-permute-start | bytes 36872 | tf_op jit(solution)/shard_map/ppermute | solution.py:17
  (14 other events, 203.2 us)
where the time goes:
time: 254 us; the launch traced here: 251 us
  blocking collectives  101 us (40%)
  starting transfers between devices  75.8 us (30%)
  local copies, waits for them, and re-layouts  51.6 us (20%)
  matrix products  14.8 us (6%)
  other arithmetic  5.38 us (2%)
    ppermute x20, starting transfers between devices, shifted(): return lax.ppermute(block, axis, route)  75.8 us
    all_gather x2, blocking collectives, apply_matrix(): lax.all_gather(block_moment[None], ('gx', 'gy'), axis=0, tiled=True)  63.8 us
    all_gather x2, blocking collectives, apply_matrix(): every_top = lax.all_gather(top_moment[None], 'gx', axis=0, tiled=True)  20.7 us
    gather x2, local copies, waits for them, and re-layouts, shards(): jnp.take(signal, order, axis=1).astype(jnp.bfloat16)  12.4 us
    psum x2, blocking collectives, apply_matrix(): top_moment = lax.psum(top_term, 'gy')  12 us
    scatter x1, local copies, waits for them, and re-layouts, shards(): smoothed = empty.at[:, order].set(first.reshape(rhs_count, -1))  11.4 us
    scatter x1, local copies, waits for them, and re-layouts, shards(): twice = empty.at[:, order].set(second.reshape(rhs_count, -1))  11.4 us
    dot_general x2, matrix products, apply_matrix(): jnp.einsum('rlns,lnst->rlt', near_rows, near_tiles, preferred_element_typ...  7.46 us
  transfers between devices with their start and end apart: 20, of which 1 were waited for; matrix products, arithmetic and copies ran while one was open for 13% of the time, Pallas kernels for 0%

commit v1 on v0

v1 whole, which is shorter than its diff:
```python
import functools

import jax
import jax.numpy as jnp
from jax import lax
from jax.experimental import pallas as pl
from jax.experimental.pallas import tpu as pltpu
from jax.sharding import PartitionSpec as P

NEAR_REACH = 2
LINK_REACH = 4
LANES = 128
ROWS = 8
AXES = ("gx", "gy", "gz")
F32 = jnp.float32
BF16 = jnp.bfloat16


def halves(a):
    high = a.astype(BF16)
    low = (a - high.astype(F32)).astype(BF16)
    return jnp.concatenate([high, low], axis=0)


def dot(a, b, transposed=False):
    dims = (((1,), (1 if transposed else 0,)), ((), ()))
    if a.dtype == BF16:
        return lax.dot_general(a, b, dims, preferred_element_type=F32)
    product = lax.dot_general(halves(a), b, dims, preferred_element_type=F32)
    return product[: a.shape[0]] + product[a.shape[0] :]


def dot_nt(a, b):
    return dot(a, b, transposed=True)


def device_index():
    index = jnp.int32(0)
    for axis in AXES:
        index = index * lax.axis_size(axis) + lax.axis_index(axis)
    return index


def permuted(read, index_row, tiles, rhs_count):
    index = jnp.broadcast_to(index_row, (ROWS, LANES))
    lane = index % LANES
    tile = index // LANES
    out = [None] * (rhs_count // ROWS)
    for t in range(tiles):
        here = tile == t
        for b in range(len(out)):
            moved = jnp.take_along_axis(read(b, t), lane, axis=1, mode="promise_in_bounds")
            out[b] = moved if t == 0 else jnp.where(here, moved, out[b])
    return jnp.concatenate(out, axis=0)


def inverse(order_ref, tiles):
    columns = lax.broadcasted_iota(jnp.int32, (LANES, LANES), 0)
    rows = lax.broadcasted_iota(jnp.int32, (tiles, LANES), 0)
    lanes = lax.broadcasted_iota(jnp.int32, (tiles, LANES), 1).astype(F32)
    total = jnp.zeros((2 * tiles, LANES), F32)
    for t in range(tiles):
        row = order_ref[t : t + 1, :]
        at_lane = jnp.where(jnp.broadcast_to(row % LANES, (LANES, LANES)) == columns, 1.0, 0.0)
        at_row = jnp.broadcast_to(row // LANES, (tiles, LANES)) == rows
        place = [jnp.where(at_row, float(t), 0.0), jnp.where(at_row, lanes, 0.0)]
        total += dot_nt(jnp.concatenate(place, axis=0).astype(BF16), at_lane.astype(BF16))
    return (total[:tiles] * LANES + total[tiles:]).astype(jnp.int32)


def upward(values, basis_ref, transfer_ref, device_transfer_ref, block_transfer_ref, outs):
    moment_ref, term_ref, core_ref, chip_ref = outs
    leaf_count = len(values)
    rank = basis_ref.shape[1]
    per_row = LANES // rank
    moments = [dot_nt(values[l], basis_ref[l]) for l in range(leaf_count)]
    for l in range(leaf_count):
        moment_ref[l] = halves(moments[l])
    packed = [
        halves(jnp.concatenate(moments[l : l + per_row], axis=1))
        for l in range(0, leaf_count, per_row)
    ]
    both = dot(jnp.concatenate(packed, axis=1), transfer_ref[...])
    own = both[: both.shape[0] // 2] + both[both.shape[0] // 2 :]
    block = dot(own, device_transfer_ref[0])
    top = dot(block, block_transfer_ref[0])
    half = top.shape[0] // 2
    term = jnp.concatenate(
        [
            jnp.concatenate([own, block], axis=1),
            jnp.concatenate([top[:half], top[half:]], axis=1),
        ],
        axis=0,
    ).astype(BF16)
    term_ref[...] = jnp.broadcast_to(term[None], term_ref.shape)

    def edge(first_value, first_moment):
        pieces = []
        for l in range(first_value, first_value + NEAR_REACH):
            pieces += [values[l][:, c : c + LANES] for c in range(0, values[l].shape[1], LANES)]
        pieces += packed[first_moment // per_row : (first_moment + LINK_REACH) // per_row]
        return jnp.concatenate(pieces, axis=0)

    low = edge(0, 0)
    high = edge(leaf_count - NEAR_REACH, leaf_count - LINK_REACH)
    even = lax.axis_index("gz") % 2 == 0
    core_ref[...] = jnp.where(even, high, low)
    chip_ref[...] = jnp.where(even, low, high)


def start_kernel(*refs):
    signal_buf, sems = refs[-2:]
    kept_count = (len(refs) - 2 - 1 - 5) // 2
    sources = refs[: 1 + kept_count]
    value_ref, *outs = refs[1 + kept_count : 6 + kept_count]
    kept = refs[6 + kept_count : -2]
    order_ref, basis_ref, transfer_ref, device_transfer_ref, block_transfer_ref = kept[:5]
    copies = [
        pltpu.make_async_copy(source, target, sems.at[i])
        for i, (source, target) in enumerate(zip(sources, (signal_buf, *kept), strict=True))
    ]
    for copy in copies:
        copy.start()
    rhs_count, point_count = signal_buf.shape
    tiles = point_count // LANES
    leaf_count, _, leaf = value_ref.shape

    def read(b, t):
        return signal_buf[b * ROWS : (b + 1) * ROWS, t * LANES : (t + 1) * LANES]

    for copy in copies[:2]:
        copy.wait()
    values = []
    for l in range(leaf_count):
        parts = [
            permuted(read, order_ref[t : t + 1, :], tiles, rhs_count)
            for t in range(l * leaf // LANES, (l + 1) * leaf // LANES)
        ]
        value = jnp.concatenate(parts, axis=1).astype(BF16)
        value_ref[l] = value
        values.append(value)
    for copy in copies[2:6]:
        copy.wait()
    upward(values, basis_ref, transfer_ref, device_transfer_ref, block_transfer_ref, outs)
    for copy in copies[6:]:
        copy.wait()


def interior_kernel(second, *refs):
    near_list_ref, leaf_links_ref, value_ref, moment_ref, coupling_ref, tiles_hbm, *refs = refs
    if second:
        leaf_ref, inverse_ref, near_ref, field_ref, edge_tiles, out_hbm, *refs = refs
        tile_buf, sems, out_buf, out_sems = refs
    else:
        order_ref, near_ref, field_ref, edge_tiles, inverse_ref, tile_buf, sems = refs
    leaf_count = value_ref.shape[0]
    rank = moment_ref.shape[2]
    inside = range(NEAR_REACH, leaf_count - NEAR_REACH)
    outside = (*range(NEAR_REACH), *range(leaf_count - NEAR_REACH, leaf_count))
    copies = [
        pltpu.make_async_copy(
            tiles_hbm.at[pl.ds(l, CHUNK)], tile_buf.at[pl.ds(l - NEAR_REACH, CHUNK)], sems.at[i]
        )
        for i, l in enumerate(inside[::CHUNK])
    ]
    for i, l in enumerate((0, leaf_count - NEAR_REACH)):
        source = tiles_hbm.at[pl.ds(l, NEAR_REACH)]
        target = edge_tiles.at[pl.ds(i * NEAR_REACH, NEAR_REACH)]
        copies.append(pltpu.make_async_copy(source, target, sems.at[len(copies)]))
    for copy in copies:
        copy.start()
    first_leaf = device_index() * leaf_count
    linked = range(LINK_REACH, leaf_count - LINK_REACH)
    store_fields(
        field_ref,
        [
            leaf_coupling(moment_ref, leaf_links_ref, coupling_ref, l, -first_leaf)
            for l in linked
        ],
    )
    if second:
        writes = put_back(reader(leaf_ref), inverse_ref, out_hbm, out_buf, out_sems)
    else:
        inverse_ref[...] = inverse(order_ref, order_ref.shape[0])
    for i, l in enumerate(inside):
        if i % CHUNK == 0:
            copies[i // CHUNK].wait()
        near_ref[i] = near_product(value_ref, near_list_ref, tile_buf, l, i, -first_leaf)
    for copy in copies[len(inside) // CHUNK :]:
        copy.wait()
    if second:
        for write in writes:
            write.wait()


def edge_kernel(
    near_list_ref, leaf_links_ref, value_ref, moment_ref, core_ref, chip_ref, coupling_ref,
    tiles_ref, near_ref, field_ref, wide_value, wide_moment
):
    leaf_count, rhs_count, leaf = value_ref.shape
    moment_rows, rank = moment_ref.shape[1:]
    per_row = LANES // rank
    even = lax.axis_index("gz") % 2 == 0
    core, chip = core_ref[...], chip_ref[...]
    above = jnp.where(even, core, chip)
    below = jnp.where(even, chip, core)
    for halo, value_at, moment_at in (
        (below, 0, 0),
        (above, NEAR_REACH + leaf_count, LINK_REACH + leaf_count),
    ):
        row = 0
        for e in range(NEAR_REACH):
            for c in range(0, leaf, LANES):
                wide_value[value_at + e, :, c : c + LANES] = halo[row : row + rhs_count]
                row += rhs_count
        for e in range(LINK_REACH):
            lane = (e % per_row) * rank
            at = row + (e // per_row) * moment_rows
            wide_moment[moment_at + e] = halo[at : at + moment_rows, lane : lane + rank]
    wide_value[NEAR_REACH : NEAR_REACH + leaf_count] = value_ref[...]
    wide_moment[LINK_REACH : LINK_REACH + leaf_count] = moment_ref[...]
    first_leaf = device_index() * leaf_count
    outside = (*range(NEAR_REACH), *range(leaf_count - NEAR_REACH, leaf_count))
    for i, l in enumerate(outside):
        near_ref[i] = near_product(
            wide_value, near_list_ref, tiles_ref, l, i, NEAR_REACH - first_leaf
        )
    outside = (*range(LINK_REACH), *range(leaf_count - LINK_REACH, leaf_count))
    store_fields(
        field_ref,
        [
            leaf_coupling(wide_moment, leaf_links_ref, coupling_ref, l, LINK_REACH - first_leaf)
            for l in outside
        ],
    )


def near_product(value_ref, near_list_ref, tiles_ref, l, slot, shift):
    sources = [value_ref[near_list_ref[k, l] + shift] for k in range(near_list_ref.shape[0])]
    return dot(jnp.concatenate(sources, axis=1), tiles_ref[slot])


def leaf_coupling(moment_ref, leaf_links_ref, coupling_ref, l, shift):
    picked = [moment_ref[leaf_links_ref[k, l] + shift] for k in range(leaf_links_ref.shape[0])]
    return coupled_halves(picked, coupling_ref[l])


def store_fields(field_ref, fields):
    rank = fields[0].shape[1]
    per_row = LANES // rank
    for i in range(0, len(fields), per_row):
        field_ref[:, i * rank : (i + per_row) * rank] = jnp.concatenate(
            fields[i : i + per_row], axis=1
        )


def coupled(picked, coupling):
    rows, rank = picked[0].shape
    product = dot(jnp.concatenate(picked, axis=0), coupling)
    total = sum(
        product[k * rows : (k + 1) * rows, k * rank : (k + 1) * rank] for k in range(len(picked))
    )
    return total


def coupled_halves(picked, coupling):
    both = coupled(picked, coupling)
    return both[: both.shape[0] // 2] + both[both.shape[0] // 2 :]


def applied(
    device_links_ref, block_links_ref, top_links_ref, term_ref, near_ref, field_ref,
    edge_near_ref, edge_field_ref, basis_ref, transfer_ref, device_transfer_ref, device_coupling_ref, block_transfer_ref,
    block_coupling_ref, top_coupling_ref
):
    leaf_count, rank, _ = basis_ref.shape
    rhs_count = near_ref.shape[1]
    gz = lax.axis_size("gz")
    under_top = gz * lax.axis_size("gy")

    def top_moment(t):
        total = sum(
            term_ref[t * under_top + j, rhs_count:, :].astype(F32) for j in range(under_top)
        )
        return jnp.concatenate([total[:, :rank], total[:, rank:]], axis=0)

    def block_moment(c):
        return sum(term_ref[c * gz + j, :rhs_count, rank:].astype(F32) for j in range(gz))

    link_count = device_links_ref.shape[1]
    top_field = coupled([top_moment(top_links_ref[0, k]) for k in range(link_count)], top_coupling_ref[0])
    block_field = coupled(
        [block_moment(block_links_ref[0, k]) for k in range(link_count)], block_coupling_ref[0]
    ) + dot_nt(top_field, block_transfer_ref[0])
    device_field = coupled(
        [term_ref[device_links_ref[0, k], :rhs_count, :rank] for k in range(link_count)],
        device_coupling_ref[0],
    ) + dot_nt(block_field, device_transfer_ref[0])
    edge = LINK_REACH * rank
    leaf_field = jnp.concatenate(
        [edge_field_ref[:, :edge], field_ref[...], edge_field_ref[:, edge:]], axis=1
    )
    field = (leaf_field + dot_nt(device_field, transfer_ref[...])).astype(BF16)
    near = [edge_near_ref[l] for l in range(NEAR_REACH)]
    near += [near_ref[l] for l in range(leaf_count - 2 * NEAR_REACH)]
    near += [edge_near_ref[l] for l in range(NEAR_REACH, 2 * NEAR_REACH)]
    return [
        near[l] + dot(field[:, l * rank : (l + 1) * rank], basis_ref[l])
        for l in range(leaf_count)
    ]


INPUTS = 15


def middle_kernel(*refs):
    ins, (first_ref, value_ref, *outs) = refs[:INPUTS], refs[INPUTS:]
    basis_ref, transfer_ref, device_transfer_ref, _, block_transfer_ref = ins[8:13]
    first = applied(*ins)
    values = []
    for l in range(len(first)):
        first_ref[l] = first[l]
        value = first[l].astype(BF16)
        value_ref[l] = value
        values.append(value)
    upward(values, basis_ref, transfer_ref, device_transfer_ref, block_transfer_ref, outs)


def put_back(read, inverse_ref, out_hbm, out_buf, sems):
    rhs_count, point_count = out_buf.shape
    tiles = point_count // LANES
    part = point_count // sems.shape[0]
    writes = []
    for t in range(tiles):
        out_buf[:, t * LANES : (t + 1) * LANES] = permuted(
            read, inverse_ref[t : t + 1, :], tiles, rhs_count
        )
        if (t + 1) * LANES % part == 0:
            columns = pl.ds((t + 1) * LANES - part, part)
            write = pltpu.make_async_copy(
                out_buf.at[:, columns], out_hbm.at[:, columns], sems.at[len(writes)]
            )
            write.start()
            writes.append(write)
    return writes


def reader(leaf_ref):
    per_leaf = leaf_ref.shape[2] // LANES

    def read(b, t):
        lane = (t % per_leaf) * LANES
        return leaf_ref[t // per_leaf, b * ROWS : (b + 1) * ROWS, lane : lane + LANES]

    return read


def end_kernel(*refs):
    ins, (inverse_ref, out_hbm, second_ref, out_buf, sems) = refs[:INPUTS], refs[INPUTS:]
    second = applied(*ins)
    for l in range(len(second)):
        second_ref[l] = second[l]
    for write in put_back(reader(second_ref), inverse_ref, out_hbm, out_buf, sems):
        write.wait()


VMEM = pl.BlockSpec(memory_space=pltpu.VMEM)
SMEM = pl.BlockSpec(memory_space=pltpu.SMEM)
HBM = pl.BlockSpec(memory_space=pltpu.HBM)
MIB = 1 << 20
CHUNK = 3
PARTS = 4


def call(kernel, name, in_specs, outs, out_specs=None, scratch=(), flops=10**6, limit=24 * MIB):
    return pl.pallas_call(
        kernel,
        name=name,
        in_specs=in_specs,
        out_specs=jax.tree.map(lambda _: VMEM, outs) if out_specs is None else out_specs,
        out_shape=outs,
        scratch_shapes=list(scratch),
        cost_estimate=pl.CostEstimate(flops=flops, bytes_accessed=MIB, transcendentals=0),
        compiler_params=pltpu.CompilerParams(vmem_limit_bytes=limit),
    )


def in_hbm(array):
    return pltpu.with_memory_space_constraint(array, pltpu.HBM)


def exchange(core, chip):
    count = 1
    for axis in AXES:
        count *= lax.axis_size(axis)
    inner = [(i, i ^ 1) for i in range(count)]
    outer = [(i, i + 1 if i % 2 else i - 1) for i in range(1, count - 1)]
    return lax.ppermute(core, AXES, inner), lax.ppermute(chip, AXES, outer)


def shards(
    signal, order, near_tiles, near_list, leaf_basis, leaf_transfer, leaf_coupling, leaf_links,
    device_transfer, device_coupling, device_links, block_transfer, block_coupling, block_links,
    top_coupling, top_links
):
    rhs_count, point_count = signal.shape
    leaf_count, rank, leaf = leaf_basis.shape
    tiles = point_count // LANES
    count = 1
    for axis in AXES:
        count *= lax.axis_size(axis)
    shape = jax.ShapeDtypeStruct
    value_out = shape((leaf_count, rhs_count, leaf), BF16)
    wide_out = shape((leaf_count, rhs_count, leaf), F32)
    points_out = shape((rhs_count, point_count), F32)
    inverse_out = shape((tiles, LANES), jnp.int32)
    halo_rows = NEAR_REACH * rhs_count * leaf // LANES + LINK_REACH * 2 * rhs_count * rank // LANES
    up_outs = (
        shape((leaf_count, 2 * rhs_count, rank), BF16),
        shape((count, rhs_count + rhs_count // 2, LANES), BF16),
        shape((halo_rows, LANES), BF16),
        shape((halo_rows, LANES), BF16),
    )
    kept = (
        order.reshape(tiles, LANES),
        leaf_basis,
        leaf_transfer.reshape(leaf_count * rank, rank),
        device_transfer,
        block_transfer,
        device_coupling,
        block_coupling,
        top_coupling,
        leaf_coupling,
    )
    near_tiles = near_tiles.reshape(leaf_count, -1, leaf)
    lists = (near_list.T, leaf_links.T, device_links, block_links, top_links)
    outs = (value_out,) + up_outs + tuple(shape(k.shape, k.dtype) for k in kept + lists)
    value, moment, term, core, chip, *kept = call(
        start_kernel,
        "start",
        [HBM] * (1 + len(kept + lists)),
        outs,
        out_specs=(VMEM,) * (5 + len(kept)) + (SMEM,) * len(lists),
        scratch=[
            pltpu.VMEM((rhs_count, point_count), F32),
            pltpu.SemaphoreType.DMA((1 + len(kept + lists),)),
        ],
    )(*map(in_hbm, (signal, *kept, *lists)))
    order, basis, transfer, device_transfer, block_transfer, *kept = kept
    device_coupling, block_coupling, top_coupling, coupling, *lists = kept
    near_list, leaf_links, *coarse_links = lists

    inside = leaf_count - 2 * NEAR_REACH
    tile_shape = near_tiles.shape[1:]
    inside_outs = (
        shape((inside, rhs_count, leaf), F32),
        shape((rhs_count, (leaf_count - 2 * LINK_REACH) * rank), F32),
        shape((2 * NEAR_REACH, *tile_shape), BF16),
    )
    edge_outs = (
        shape((2 * NEAR_REACH, rhs_count, leaf), F32),
        shape((rhs_count, 2 * LINK_REACH * rank), F32),
    )
    tile_scratch = [
        pltpu.VMEM((inside, *tile_shape), BF16),
        pltpu.SemaphoreType.DMA((inside // CHUNK + 2,)),
    ]
    out_scratch = [pltpu.VMEM((rhs_count, point_count), F32), pltpu.SemaphoreType.DMA((PARTS,))]
    edge_scratch = [
        pltpu.VMEM((leaf_count + 2 * NEAR_REACH, rhs_count, leaf), BF16),
        pltpu.VMEM((leaf_count + 2 * LINK_REACH, 2 * rhs_count, rank), BF16),
    ]

    def interior(second, last_out, out_spec, scratch, *more):
        return call(
            functools.partial(interior_kernel, second),
            "interior_second" if second else "interior_first",
            [SMEM] * 2 + [VMEM] * 3 + [HBM] + [VMEM] * len(more),
            inside_outs + (last_out,),
            out_specs=(VMEM,) * 3 + (out_spec,),
            scratch=scratch,
            flops=10**8,
        )(near_list, leaf_links, value, moment, coupling, in_hbm(near_tiles), *more)

    def edges(tiles):
        return call(edge_kernel, "edges", [SMEM] * 2 + [VMEM] * 6, edge_outs, scratch=edge_scratch)(
            near_list, leaf_links, value, moment, core, chip, coupling, tiles
        )

    def spread(term):
        return lax.all_to_all(term, AXES, 0, 0)

    coarse = (
        basis, transfer, device_transfer, device_coupling, block_transfer, block_coupling,
        top_coupling,
    )
    core, chip = exchange(core, chip)
    term = spread(term)
    near, field, tiles, inverse_order = interior(False, inverse_out, VMEM, tile_scratch, order)
    edge_near, edge_field = edges(tiles)
    first, value, moment, term, core, chip = call(
        middle_kernel, "middle", [SMEM] * 3 + [VMEM] * 12, (wide_out, value_out) + up_outs
    )(*coarse_links, term, near, field, edge_near, edge_field, *coarse)
    core, chip = exchange(core, chip)
    term = spread(term)
    near, field, tiles, smoothed = interior(
        True, points_out, HBM, tile_scratch + out_scratch, first, inverse_order
    )
    edge_near, edge_field = edges(tiles)
    twice = call(
        end_kernel, "end", [SMEM] * 3 + [VMEM] * 13, points_out, out_specs=HBM,
        scratch=[pltpu.VMEM(wide_out.shape, F32)] + out_scratch,
    )(*coarse_links, term, near, field, edge_near, edge_field, *coarse, inverse_order)
    return smoothed, twice


def solution(mesh):
    every = ("gx", "gy", "gz")
    in_specs = (
        P(None, every),
        P(every),
        P(every, None, None, None),
        P(every, None),
        P(every, None, None),
        P(every, None, None),
        P(every, None, None),
        P(every, None),
        P(every, None, None),
        P(every, None, None),
        P(every, None),
        P(("gx", "gy"), None, None),
        P(("gx", "gy"), None, None),
        P(("gx", "gy"), None),
        P("gx", None, None),
        P("gx", None),
    )
    out_specs = (P(None, every), P(None, every))
    return jax.shard_map(shards, mesh=mesh, in_specs=in_specs, out_specs=out_specs, check_vma=False)
```

time: 254 us -> 43.8 us (0.17)
  blocking collectives: 101 us -> 0 us
  starting transfers between devices: 75.8 us -> 19.2 us
  local copies, waits for them, and re-layouts: 51.6 us -> 0 us
  Pallas kernels: 0 us -> 23.5 us
  matrix products: 14.8 us -> 0 us
  other arithmetic: 5.38 us -> 0 us
    all_gather x4 -> x0, blocking collectives: 84.5 us -> none  [the longest x2 63.8 us: apply_matrix(): lax.all_gather(block_moment[None], ('gx', 'gy'), axis=0, tiled=True)]
    ppermute x20 -> x4, starting transfers between devices: 75.8 us -> 7.42 us  [exchange(): return (lax.ppermute(core, AXES, inner), lax.ppermute(chip, AXES, outer))]
    pallas_call x0 -> x7, Pallas kernels: none -> 23.5 us  [the longest x2 9.3 us: interior(): call(functools.partial(interior_kernel, second), 'interior_second' if sec...]
    scatter x2 -> x0, local copies, waits for them, and re-layouts: 22.8 us -> none  [the longest x1 11.4 us: shards(): smoothed = empty.at[:, order].set(first.reshape(rhs_count, -1))]
    gather x12 -> x0, local copies, waits for them, and re-layouts: 18.3 us -> none  [the longest x2 12.4 us: shards(): jnp.take(signal, order, axis=1).astype(jnp.bfloat16)]
    psum x4 -> x0, blocking collectives: 17 us -> none  [the longest x2 12 us: apply_matrix(): top_moment = lax.psum(top_term, 'gy')]
    dot_general x26 -> x0, matrix products: 14.8 us -> none  [the longest x2 7.46 us: apply_matrix(): jnp.einsum('rlns,lnst->rlt', near_rows, near_tiles, preferred_element_typ...]
    all_to_all x0 -> x2, starting transfers between devices: none -> 11.8 us  [spread(): return lax.all_to_all(term, AXES, 0, 0)]
  transfers between devices with their start and end apart: 20 -> 6, of which waited for: 1 -> 0; matrix products, arithmetic and copies ran while one was open for 13% -> 0% of each run, Pallas kernels for 0% -> 27%
where the time goes in v1:
time: 43.8 us; the launch traced here: 43.5 us
  Pallas kernels  23.5 us (54%)
  starting transfers between devices  19.2 us (44%)
  between operations  0.73 us (2%)
    all_to_all x2, starting transfers between devices, spread(): return lax.all_to_all(term, AXES, 0, 0)  11.8 us
    pallas_call x2, Pallas kernels, interior(): call(functools.partial(interior_kernel, second), 'interior_second' if sec...  9.3 us
    ppermute x4, starting transfers between devices, exchange(): return (lax.ppermute(core, AXES, inner), lax.ppermute(chip, AXES, outer))  7.42 us
    pallas_call x1, Pallas kernels, shards(): call(end_kernel, 'end', [SMEM] * 3 + [VMEM] * 13, points_out, out_specs=H...  5.16 us
    pallas_call x1, Pallas kernels, shards(): call(start_kernel, 'start', [HBM] * (1 + len(kept + lists)), outs, out_sp...  3.9 us
    pallas_call x1, Pallas kernels, shards(): call(middle_kernel, 'middle', [SMEM] * 3 + [VMEM] * 12, (wide_out, value_...  2.83 us
    pallas_call x2, Pallas kernels, edges(): call(edge_kernel, 'edges', [SMEM] * 2 + [VMEM] * 6, edge_outs, scratch=ed...  2.35 us
  transfers between devices with their start and end apart: 6, of which 0 were waited for; matrix products, arithmetic and copies ran while one was open for 0% of the time, Pallas kernels for 27%

profile of v1, /device:TPU:1, one launch (start us, length us, event | category | flops | bytes accessed | tf_op | source)
XLA Modules:
  0.0 43.5 jit_solution(10742730640703705368)
XLA Ops:
  0.6 3.9 %start.1 = (bf16[16,16,256]{2,1,0:T(8,128)(2,1)S(1)}, bf16[16,32,64]{2,1,0:T(8,128)(2,1)S(1)}, bf16[32,24,128]{2,1,0:T(8,128)(2,1)}, bf16[128,128]{1,0:T(8,128)(...) custom-call(f32[16,4096]{1,0:T(8,128)} %refs_0_.1, ...), custom_call_target="tpu_custom_call" | custom-call | flops 1000000 | bytes 1048576 | tf_op jit(solution)/shard_map/start/pallas_call | solution.py:438
  4.5 7.1 %all-to-all-start = ((bf16[32,24,128]{2,1,0:T(8,128)(2,1)}), bf16[32,24,128]{2,1,0:T(8,128)(2,1)S(1)}, u32[]{:S(2)}, u32[]{:S(2)}) async-start(bf16[32,24,128]{2,1,0:T(8,128)(2,1)} %get-tuple-element.44), calls=%async_computation | async-start | bytes 393216 | tf_op jit(solution)/shard_map/all_to_all | solution.py:491
  11.6 0.3 collective-permute-start
  12.0 3.4 %collective-permute-start.1 = (bf16[128,128]{1,0:T(8,128)(2,1)S(1)}, bf16[128,128]{1,0:T(8,128)(2,1)S(1)}, u32[]{:S(2)}, u32[]{:S(2)}) collective-permute-start(bf16[128,128]{1,0:T(8,128)(2,1)S(1)} %get-tuple-element.52), channel_id=1, source_target_pairs={{1,2},{2,1},{3,4},{4,3},{5,6},{6,5},{7,8},{8,7},{9,10},{10,9},{11,... | collective-permute-start | bytes 98312 | tf_op jit(solution)/shard_map/ppermute | solution.py:398
  15.4 4.6 %interior_first.1 = (f32[12,16,256]{2,1,0:T(8,128)S(1)}, f32[16,512]{1,0:T(8,128)S(1)}, bf16[4,768,256]{2,1,0:T(8,128)(2,1)S(1)}, s32[32,128]{1,0:T(8,128)S(1)}) custom-call(s32[3,16]{1,0:T(4,128)S(1)} %get-tuple-element.39.refs_0_.near_list_ref, s32[3,16]{1,0:T(4,128)S(1)} %get-tuple-element.40.refs_1_.leaf_links_ref, ...), custom_call_target="tpu_custom_call" | custom-call | flops 100000000 | bytes 1048576 | tf_op jit(solution)/shard_map/interior_first/pallas_call | solution.py:475
  19.9 0.0 collective-permute-done.core_ref
  19.9 0.0 collective-permute-done.1.chip_ref
  19.9 1.2 %edges.2 = (f32[4,16,256]{2,1,0:T(8,128)S(1)}, f32[16,512]{1,0:T(8,128)S(1)}) custom-call(s32[3,16]{1,0:T(4,128)S(1)} %get-tuple-element.39.refs_0_.near_list_ref, s32[3,16]{1,0:T(4,128)S(1)} %get-tuple-element.40.refs_1_.leaf_links_ref, bf16[16,16,256]{2,1,0:T(8,128)(2,1)S(1)} %get-tuple-element.45.refs_2_.value_ref, ...), custom_call_target="tpu_custom_call" | custom-call | flops 1000000 | bytes 1048576 | tf_op jit(solution)/shard_map/edges/pallas_call | solution.py:486
  21.1 0.0 all-to-all-done.refs_3_
  21.1 2.8 %middle.1 = (f32[16,16,256]{2,1,0:T(8,128)S(1)}, bf16[16,16,256]{2,1,0:T(8,128)(2,1)S(1)}, bf16[16,32,64]{2,1,0:T(8,128)(2,1)S(1)}, bf16[32,24,128]{2,1,0:T(8,12...) custom-call(s32[1,3]{1,0:T(1,128)S(1)} %get-tuple-element.41.refs_0_, ...), custom_call_target="tpu_custom_call" | custom-call | flops 1000000 | bytes 1048576 | tf_op jit(solution)/shard_map/middle/pallas_call | solution.py:501
  23.9 4.7 %all-to-all-start.1 = ((bf16[32,24,128]{2,1,0:T(8,128)(2,1)}), bf16[32,24,128]{2,1,0:T(8,128)(2,1)S(1)}, u32[]{:S(2)}, u32[]{:S(2)}) async-start(bf16[32,24,128]{2,1,0:T(8,128)(2,1)} %get-tuple-element.68), calls=%async_computation.1 | async-start | bytes 393216 | tf_op jit(solution)/shard_map/all_to_all | solution.py:491
  28.7 0.3 collective-permute-start.2
  29.0 3.4 %collective-permute-start.3 = (bf16[128,128]{1,0:T(8,128)(2,1)S(1)}, bf16[128,128]{1,0:T(8,128)(2,1)S(1)}, u32[]{:S(2)}, u32[]{:S(2)}) collective-permute-start(bf16[128,128]{1,0:T(8,128)(2,1)S(1)} %get-tuple-element.72), channel_id=1, source_target_pairs={{1,2},{2,1},{3,4},{4,3},{5,6},{6,5},{7,8},{8,7},{9,10},{10,9},{11,... | collective-permute-start | bytes 98312 | tf_op jit(solution)/shard_map/ppermute | solution.py:398
  32.4 4.7 %interior_second.1 = (f32[12,16,256]{2,1,0:T(8,128)S(1)}, f32[16,512]{1,0:T(8,128)S(1)}, bf16[4,768,256]{2,1,0:T(8,128)(2,1)S(1)}, f32[16,4096]{1,0:T(8,128)}) custom-call(s32[3,16]{1,0:T(4,128)S(1)} %get-tuple-element.39.refs_0_.near_list_ref, s32[3,16]{1,0:T(4,128)S(1)} %get-tuple-element.40.refs_1_.leaf_links_ref, ...), custom_call_target="tpu_custom_call" | custom-call | flops 100000000 | bytes 1048576 | tf_op jit(solution)/shard_map/interior_second/pallas_call | solution.py:475
  37.2 0.0 collective-permute-done.2.core_ref
  37.2 0.0 collective-permute-done.3.chip_ref
  37.2 1.2 %edges.3 = (f32[4,16,256]{2,1,0:T(8,128)S(1)}, f32[16,512]{1,0:T(8,128)S(1)}) custom-call(s32[3,16]{1,0:T(4,128)S(1)} %get-tuple-element.39.refs_0_.near_list_ref, s32[3,16]{1,0:T(4,128)S(1)} %get-tuple-element.40.refs_1_.leaf_links_ref, bf16[16,16,256]{2,1,0:T(8,128)(2,1)S(1)} %get-tuple-element.63.refs_2_.value_ref, ...), custom_call_target="tpu_custom_call" | custom-call | flops 1000000 | bytes 1048576 | tf_op jit(solution)/shard_map/edges/pallas_call | solution.py:486
  38.4 0.0 all-to-all-done.1.refs_3_
  38.4 5.2 %end.1 = f32[16,4096]{1,0:T(8,128)} custom-call(s32[1,3]{1,0:T(1,128)S(1)} %get-tuple-element.41.refs_0_, s32[1,3]{1,0:T(1,128)S(1)} %get-tuple-element.42.refs_1_, s32[1,3]{1,0:T(1,128)S(1)} %get-tuple-element.43.refs_2_, bf16[32,24,128]{2,1,0:T(8,128)(2,1)S(1)} %all-to-all-done.1.refs_3_, f32[12,16,256]{2,1,0:T(8,128)S(1)} %get-tuple-element.69.refs_4_, ...), custom_call_target="tpu_custom_call" | custom-call | flops 1000000 | bytes 1048576 | tf_op jit(solution)/shard_map/end/pallas_call | solution.py:510
Async XLA Ops:
  4.5 16.6 %all-to-all-start = ((bf16[32,24,128]{2,1,0:T(8,128)(2,1)}), bf16[32,24,128]{2,1,0:T(8,128)(2,1)S(1)}, u32[]{:S(2)}, u32[]{:S(2)}) async-start(bf16[32,24,128]{2,1,0:T(8,128)(2,1)} %get-tuple-element.44), calls=%async_computation | async-start | bytes 393216 | tf_op jit(solution)/shard_map/all_to_all | solution.py:491
  11.6 8.3 %collective-permute-start = (bf16[128,128]{1,0:T(8,128)(2,1)S(1)}, bf16[128,128]{1,0:T(8,128)(2,1)S(1)}, u32[]{:S(2)}, u32[]{:S(2)}) collective-permute-start(bf16[128,128]{1,0:T(8,128)(2,1)S(1)} %get-tuple-element.51), channel_id=1, source_target_pairs={{0,1},{1,0},{2,3},{3,2},{4,5},{5,4},{6,7},{7,6},{8,9},{9,8},{10,11... | collective-permute-start | bytes 98312 | tf_op jit(solution)/shard_map/ppermute | solution.py:398
  12.0 8.0 %collective-permute-start.1 = (bf16[128,128]{1,0:T(8,128)(2,1)S(1)}, bf16[128,128]{1,0:T(8,128)(2,1)S(1)}, u32[]{:S(2)}, u32[]{:S(2)}) collective-permute-start(bf16[128,128]{1,0:T(8,128)(2,1)S(1)} %get-tuple-element.52), channel_id=1, source_target_pairs={{1,2},{2,1},{3,4},{4,3},{5,6},{6,5},{7,8},{8,7},{9,10},{10,9},{11,... | collective-permute-start | bytes 98312 | tf_op jit(solution)/shard_map/ppermute | solution.py:398
  23.9 14.4 %all-to-all-start.1 = ((bf16[32,24,128]{2,1,0:T(8,128)(2,1)}), bf16[32,24,128]{2,1,0:T(8,128)(2,1)S(1)}, u32[]{:S(2)}, u32[]{:S(2)}) async-start(bf16[32,24,128]{2,1,0:T(8,128)(2,1)} %get-tuple-element.68), calls=%async_computation.1 | async-start | bytes 393216 | tf_op jit(solution)/shard_map/all_to_all | solution.py:491
  28.7 8.5 %collective-permute-start.2 = (bf16[128,128]{1,0:T(8,128)(2,1)S(1)}, bf16[128,128]{1,0:T(8,128)(2,1)S(1)}, u32[]{:S(2)}, u32[]{:S(2)}) collective-permute-start(bf16[128,128]{1,0:T(8,128)(2,1)S(1)} %get-tuple-element.71), channel_id=1, source_target_pairs={{0,1},{1,0},{2,3},{3,2},{4,5},{5,4},{6,7},{7,6},{8,9},{9,8},{10,11... | collective-permute-start | bytes 98312 | tf_op jit(solution)/shard_map/ppermute | solution.py:398
  29.0 8.2 %collective-permute-start.3 = (bf16[128,128]{1,0:T(8,128)(2,1)S(1)}, bf16[128,128]{1,0:T(8,128)(2,1)S(1)}, u32[]{:S(2)}, u32[]{:S(2)}) collective-permute-start(bf16[128,128]{1,0:T(8,128)(2,1)S(1)} %get-tuple-element.72), channel_id=1, source_target_pairs={{1,2},{2,1},{3,4},{4,3},{5,6},{6,5},{7,8},{8,7},{9,10},{10,9},{11,... | collective-permute-start | bytes 98312 | tf_op jit(solution)/shard_map/ppermute | solution.py:398

commit v2 on v1

--- a/solution.py
+++ b/solution.py
@@ -41,7 +41,7 @@
     return index
 
 
-def permuted(read, index_row, tiles, rhs_count):
+def moved_lanes(read, index_row, tiles, rhs_count):
     index = jnp.broadcast_to(index_row, (ROWS, LANES))
     lane = index % LANES
     tile = index // LANES
@@ -52,6 +52,41 @@
             moved = jnp.take_along_axis(read(b, t), lane, axis=1, mode="promise_in_bounds")
             out[b] = moved if t == 0 else jnp.where(here, moved, out[b])
     return jnp.concatenate(out, axis=0)
+
+
+def selected_lanes(table_ref, index_rows, tiles, rhs_count):
+    columns = lax.broadcasted_iota(jnp.int32, (LANES, LANES), 0)
+    chosen = jnp.concatenate(
+        [
+            jnp.where(jnp.broadcast_to(row % LANES, (LANES, LANES)) == columns, 1.0, 0.0).astype(BF16)
+            for row in index_rows
+        ],
+        axis=1,
+    )
+    chosen = jnp.concatenate([chosen] * (table_ref.shape[1] // LANES), axis=0)
+    tile = jnp.concatenate(
+        [jnp.broadcast_to(row // LANES, (rhs_count, LANES)) for row in index_rows], axis=1
+    )
+    out = jnp.zeros(tile.shape, F32)
+    for first in range(0, tiles, TILE_GROUP):
+        rows = table_ref[first * rhs_count : (first + TILE_GROUP) * rhs_count]
+        moved = dot(rows, chosen)
+        for t in range(TILE_GROUP):
+            part = moved[t * rhs_count : (t + 1) * rhs_count]
+            out = jnp.where(tile == first + t, part, out)
+    return out
+
+
+def permuted(read, index_ref, table_ref, pattern, rhs_count):
+    tiles = index_ref.shape[0]
+    for pair in range(tiles // 2):
+        rows = [index_ref[t : t + 1, :] for t in (2 * pair, 2 * pair + 1)]
+        if pattern[pair % len(pattern)]:
+            yield selected_lanes(table_ref, rows, tiles, rhs_count)
+        else:
+            yield jnp.concatenate(
+                [moved_lanes(read, row, tiles, rhs_count) for row in rows], axis=1
+            )
 
 
 def inverse(order_ref, tiles):
@@ -74,8 +109,6 @@
     rank = basis_ref.shape[1]
     per_row = LANES // rank
     moments = [dot_nt(values[l], basis_ref[l]) for l in range(leaf_count)]
-    for l in range(leaf_count):
-        moment_ref[l] = halves(moments[l])
     packed = [
         halves(jnp.concatenate(moments[l : l + per_row], axis=1))
         for l in range(0, leaf_count, per_row)
@@ -93,6 +126,8 @@
         axis=0,
     ).astype(BF16)
     term_ref[...] = jnp.broadcast_to(term[None], term_ref.shape)
+    for l in range(leaf_count):
+        moment_ref[l] = halves(moments[l])
 
     def edge(first_value, first_moment):
         pieces = []
@@ -115,15 +150,15 @@
     value_ref, *outs = refs[1 + kept_count : 6 + kept_count]
     kept = refs[6 + kept_count : -2]
     order_ref, basis_ref, transfer_ref, device_transfer_ref, block_transfer_ref = kept[:5]
+    rhs_count, point_count = signal_buf.shape
+    tiles = point_count // LANES
+    leaf_count, _, leaf = value_ref.shape
     copies = [
         pltpu.make_async_copy(source, target, sems.at[i])
         for i, (source, target) in enumerate(zip(sources, (signal_buf, *kept), strict=True))
     ]
     for copy in copies:
         copy.start()
-    rhs_count, point_count = signal_buf.shape
-    tiles = point_count // LANES
-    leaf_count, _, leaf = value_ref.shape
 
     def read(b, t):
         return signal_buf[b * ROWS : (b + 1) * ROWS, t * LANES : (t + 1) * LANES]
@@ -133,7 +168,7 @@
     values = []
     for l in range(leaf_count):
         parts = [
-            permuted(read, order_ref[t : t + 1, :], tiles, rhs_count)
+            moved_lanes(read, order_ref[t : t + 1, :], tiles, rhs_count)
             for t in range(l * leaf // LANES, (l + 1) * leaf // LANES)
         ]
         value = jnp.concatenate(parts, axis=1).astype(BF16)
@@ -141,7 +176,9 @@
         values.append(value)
     for copy in copies[2:6]:
         copy.wait()
-    upward(values, basis_ref, transfer_ref, device_transfer_ref, block_transfer_ref, outs)
+    upward(
+        values, basis_ref, transfer_ref, device_transfer_ref, block_transfer_ref, outs
+    )
     for copy in copies[6:]:
         copy.wait()
 
@@ -150,13 +187,11 @@
     near_list_ref, leaf_links_ref, value_ref, moment_ref, coupling_ref, tiles_hbm, *refs = refs
     if second:
         leaf_ref, inverse_ref, near_ref, field_ref, edge_tiles, out_hbm, *refs = refs
-        tile_buf, sems, out_buf, out_sems = refs
+        tile_buf, sems, table_ref, out_buf, out_sems = refs
     else:
         order_ref, near_ref, field_ref, edge_tiles, inverse_ref, tile_buf, sems = refs
     leaf_count = value_ref.shape[0]
-    rank = moment_ref.shape[2]
     inside = range(NEAR_REACH, leaf_count - NEAR_REACH)
-    outside = (*range(NEAR_REACH), *range(leaf_count - NEAR_REACH, leaf_count))
     copies = [
         pltpu.make_async_copy(
             tiles_hbm.at[pl.ds(l, CHUNK)], tile_buf.at[pl.ds(l - NEAR_REACH, CHUNK)], sems.at[i]
@@ -167,7 +202,7 @@
         source = tiles_hbm.at[pl.ds(l, NEAR_REACH)]
         target = edge_tiles.at[pl.ds(i * NEAR_REACH, NEAR_REACH)]
         copies.append(pltpu.make_async_copy(source, target, sems.at[len(copies)]))
-    for copy in copies:
+    for copy in (*copies[len(inside) // CHUNK :], *copies[: len(inside) // CHUNK]):
         copy.start()
     first_leaf = device_index() * leaf_count
     linked = range(LINK_REACH, leaf_count - LINK_REACH)
@@ -179,7 +214,8 @@
         ],
     )
     if second:
-        writes = put_back(reader(leaf_ref), inverse_ref, out_hbm, out_buf, out_sems)
+        values = [leaf_ref[l] for l in range(leaf_count)]
+        writes = put_back(values, leaf_ref, inverse_ref, out_hbm, table_ref, out_buf, out_sems)
     else:
         inverse_ref[...] = inverse(order_ref, order_ref.shape[0])
     for i, l in enumerate(inside):
@@ -317,50 +353,50 @@
     ins, (first_ref, value_ref, *outs) = refs[:INPUTS], refs[INPUTS:]
     basis_ref, transfer_ref, device_transfer_ref, _, block_transfer_ref = ins[8:13]
     first = applied(*ins)
-    values = []
+    values = [leaf_first.astype(BF16) for leaf_first in first]
+    upward(values, basis_ref, transfer_ref, device_transfer_ref, block_transfer_ref, outs)
     for l in range(len(first)):
         first_ref[l] = first[l]
-        value = first[l].astype(BF16)
-        value_ref[l] = value
-        values.append(value)
-    upward(values, basis_ref, transfer_ref, device_transfer_ref, block_transfer_ref, outs)
-
-
-def put_back(read, inverse_ref, out_hbm, out_buf, sems):
+        value_ref[l] = values[l]
+
+
+def put_back(values, leaf_ref, inverse_ref, out_hbm, table_ref, out_buf, sems):
     rhs_count, point_count = out_buf.shape
-    tiles = point_count // LANES
+    per_leaf = leaf_ref.shape[2] // LANES
     part = point_count // sems.shape[0]
+    for l in range(len(values)):
+        for c in range(per_leaf):
+            value = values[l][:, c * LANES : (c + 1) * LANES]
+            high = value.astype(BF16)
+            low = (value - high.astype(F32)).astype(BF16)
+            row = (l * per_leaf + c) * rhs_count
+            table_ref[row : row + rhs_count] = jnp.concatenate([high, low], axis=1)
+
+    def read(b, t):
+        lane = (t % per_leaf) * LANES
+        return leaf_ref[t // per_leaf, b * ROWS : (b + 1) * ROWS, lane : lane + LANES]
+
     writes = []
-    for t in range(tiles):
-        out_buf[:, t * LANES : (t + 1) * LANES] = permuted(
-            read, inverse_ref[t : t + 1, :], tiles, rhs_count
-        )
-        if (t + 1) * LANES % part == 0:
-            columns = pl.ds((t + 1) * LANES - part, part)
+    end = 0
+    for columns in permuted(read, inverse_ref, table_ref, (True, True, False), rhs_count):
+        start, end = end, end + columns.shape[1]
+        out_buf[:, start:end] = columns
+        if end % part == 0:
+            written = pl.ds(end - part, part)
             write = pltpu.make_async_copy(
-                out_buf.at[:, columns], out_hbm.at[:, columns], sems.at[len(writes)]
+                out_buf.at[:, written], out_hbm.at[:, written], sems.at[len(writes)]
             )
             write.start()
             writes.append(write)
     return writes
 
 
-def reader(leaf_ref):
-    per_leaf = leaf_ref.shape[2] // LANES
-
-    def read(b, t):
-        lane = (t % per_leaf) * LANES
-        return leaf_ref[t // per_leaf, b * ROWS : (b + 1) * ROWS, lane : lane + LANES]
-
-    return read
-
-
 def end_kernel(*refs):
-    ins, (inverse_ref, out_hbm, second_ref, out_buf, sems) = refs[:INPUTS], refs[INPUTS:]
+    ins, (inverse_ref, out_hbm, second_ref, *scratch) = refs[:INPUTS], refs[INPUTS:]
     second = applied(*ins)
     for l in range(len(second)):
         second_ref[l] = second[l]
-    for write in put_back(reader(second_ref), inverse_ref, out_hbm, out_buf, sems):
+    for write in put_back(second, second_ref, inverse_ref, out_hbm, *scratch):
         write.wait()
 
 
@@ -368,8 +404,9 @@
 SMEM = pl.BlockSpec(memory_space=pltpu.SMEM)
 HBM = pl.BlockSpec(memory_space=pltpu.HBM)
 MIB = 1 << 20
-CHUNK = 3
+CHUNK = 4
 PARTS = 4
+TILE_GROUP = 8
 
 
 def call(kernel, name, in_specs, outs, out_specs=None, scratch=(), flops=10**6, limit=24 * MIB):
@@ -395,7 +432,8 @@
         count *= lax.axis_size(axis)
     inner = [(i, i ^ 1) for i in range(count)]
     outer = [(i, i + 1 if i % 2 else i - 1) for i in range(1, count - 1)]
-    return lax.ppermute(core, AXES, inner), lax.ppermute(chip, AXES, outer)
+    chip = lax.ppermute(chip, AXES, outer)
+    return lax.ppermute(core, AXES, inner), chip
 
 
 def shards(
@@ -405,7 +443,7 @@
 ):
     rhs_count, point_count = signal.shape
     leaf_count, rank, leaf = leaf_basis.shape
-    tiles = point_count // LANES
+    column_tiles = point_count // LANES
     count = 1
     for axis in AXES:
         count *= lax.axis_size(axis)
@@ -413,7 +451,7 @@
     value_out = shape((leaf_count, rhs_count, leaf), BF16)
     wide_out = shape((leaf_count, rhs_count, leaf), F32)
     points_out = shape((rhs_count, point_count), F32)
-    inverse_out = shape((tiles, LANES), jnp.int32)
+    inverse_out = shape((column_tiles, LANES), jnp.int32)
     halo_rows = NEAR_REACH * rhs_count * leaf // LANES + LINK_REACH * 2 * rhs_count * rank // LANES
     up_outs = (
         shape((leaf_count, 2 * rhs_count, rank), BF16),
@@ -422,7 +460,7 @@
         shape((halo_rows, LANES), BF16),
     )
     kept = (
-        order.reshape(tiles, LANES),
+        order.reshape(column_tiles, LANES),
         leaf_basis,
         leaf_transfer.reshape(leaf_count * rank, rank),
         device_transfer,
@@ -434,6 +472,7 @@
     )
     near_tiles = near_tiles.reshape(leaf_count, -1, leaf)
     lists = (near_list.T, leaf_links.T, device_links, block_links, top_links)
+    tile_shape = near_tiles.shape[1:]
     outs = (value_out,) + up_outs + tuple(shape(k.shape, k.dtype) for k in kept + lists)
     value, moment, term, core, chip, *kept = call(
         start_kernel,
@@ -451,7 +490,6 @@
     near_list, leaf_links, *coarse_links = lists
 
     inside = leaf_count - 2 * NEAR_REACH
-    tile_shape = near_tiles.shape[1:]
     inside_outs = (
         shape((inside, rhs_count, leaf), F32),
         shape((rhs_count, (leaf_count - 2 * LINK_REACH) * rank), F32),
@@ -465,7 +503,11 @@
         pltpu.VMEM((inside, *tile_shape), BF16),
         pltpu.SemaphoreType.DMA((inside // CHUNK + 2,)),
     ]
-    out_scratch = [pltpu.VMEM((rhs_count, point_count), F32), pltpu.SemaphoreType.DMA((PARTS,))]
+    out_scratch = [
+        pltpu.VMEM((column_tiles * rhs_count, 2 * LANES), BF16),
+        pltpu.VMEM((rhs_count, point_count), F32),
+        pltpu.SemaphoreType.DMA((PARTS,)),
+    ]
     edge_scratch = [
         pltpu.VMEM((leaf_count + 2 * NEAR_REACH, rhs_count, leaf), BF16),
         pltpu.VMEM((leaf_count + 2 * LINK_REACH, 2 * rhs_count, rank), BF16),
@@ -499,7 +541,7 @@
     near, field, tiles, inverse_order = interior(False, inverse_out, VMEM, tile_scratch, order)
     edge_near, edge_field = edges(tiles)
     first, value, moment, term, core, chip = call(
-        middle_kernel, "middle", [SMEM] * 3 + [VMEM] * 12, (wide_out, value_out) + up_outs
+        middle_kernel, "middle", [SMEM] * 3 + [VMEM] * 12, (wide_out, value_out) + up_outs,
     )(*coarse_links, term, near, field, edge_near, edge_field, *coarse)
     core, chip = exchange(core, chip)
     term = spread(term)

time: 43.8 us -> 41.9 us (0.957)
  Pallas kernels: 23.5 us -> 21.6 us
    pallas_call x1, Pallas kernels: 5.16 us -> 3.64 us  [shards(): call(end_kernel, 'end', [SMEM] * 3 + [VMEM] * 13, points_out, out_specs=H...]
  transfers between devices with their start and end apart: 6 -> 6, of which waited for: 0 -> 1; matrix products, arithmetic and copies ran while one was open for 0% -> 0% of each run, Pallas kernels for 27% -> 27%
where the time goes in v2:
time: 41.9 us; the launch traced here: 41.6 us
  Pallas kernels  21.6 us (52%)
  starting transfers between devices  19.1 us (46%)
  between operations  0.73 us (2%)
    all_to_all x2, starting transfers between devices, spread(): return lax.all_to_all(term, AXES, 0, 0)  11.7 us
    pallas_call x2, Pallas kernels, interior(): call(functools.partial(interior_kernel, second), 'interior_second' if sec...  8.9 us
    ppermute x2, starting transfers between devices, exchange(): chip = lax.ppermute(chip, AXES, outer)  6.77 us
    pallas_call x1, Pallas kernels, shards(): call(start_kernel, 'start', [HBM] * (1 + len(kept + lists)), outs, out_sp...  3.9 us
    pallas_call x1, Pallas kernels, shards(): call(end_kernel, 'end', [SMEM] * 3 + [VMEM] * 13, points_out, out_specs=H...  3.64 us
    pallas_call x1, Pallas kernels, shards(): call(middle_kernel, 'middle', [SMEM] * 3 + [VMEM] * 12, (wide_out, value_...  2.82 us
    pallas_call x2, Pallas kernels, edges(): call(edge_kernel, 'edges', [SMEM] * 2 + [VMEM] * 6, edge_outs, scratch=ed...  2.35 us
  transfers between devices with their start and end apart: 6, of which 1 were waited for; matrix products, arithmetic and copies ran while one was open for 0% of the time, Pallas kernels for 27%

profile of v2, /device:TPU:1, one launch (start us, length us, event | category | flops | bytes accessed | tf_op | source)
XLA Modules:
  0.0 41.6 jit_solution(3210625469724210380)
XLA Ops:
  0.6 3.9 %start.1 = (bf16[16,16,256]{2,1,0:T(8,128)(2,1)S(1)}, bf16[16,32,64]{2,1,0:T(8,128)(2,1)S(1)}, bf16[32,24,128]{2,1,0:T(8,128)(2,1)}, bf16[128,128]{1,0:T(8,128)(...) custom-call(f32[16,4096]{1,0:T(8,128)} %refs_0_.1, ...), custom_call_target="tpu_custom_call" | custom-call | flops 1000000 | bytes 1048576 | tf_op jit(solution)/shard_map/start/pallas_call | solution.py:477
  4.5 7.1 %all-to-all-start = ((bf16[32,24,128]{2,1,0:T(8,128)(2,1)}), bf16[32,24,128]{2,1,0:T(8,128)(2,1)S(1)}, u32[]{:S(2)}, u32[]{:S(2)}) async-start(bf16[32,24,128]{2,1,0:T(8,128)(2,1)} %get-tuple-element.44), calls=%async_computation | async-start | bytes 393216 | tf_op jit(solution)/shard_map/all_to_all | solution.py:533
  11.6 0.3 collective-permute-start
  12.0 3.4 %collective-permute-start.1 = (bf16[128,128]{1,0:T(8,128)(2,1)S(1)}, bf16[128,128]{1,0:T(8,128)(2,1)S(1)}, u32[]{:S(2)}, u32[]{:S(2)}) collective-permute-start(bf16[128,128]{1,0:T(8,128)(2,1)S(1)} %get-tuple-element.52), channel_id=1, source_target_pairs={{1,2},{2,1},{3,4},{4,3},{5,6},{6,5},{7,8},{8,7},{9,10},{10,9},{11,... | collective-permute-start | bytes 98312 | tf_op jit(solution)/shard_map/ppermute | solution.py:435
  15.4 4.1 %interior_first.1 = (f32[12,16,256]{2,1,0:T(8,128)S(1)}, f32[16,512]{1,0:T(8,128)S(1)}, bf16[4,768,256]{2,1,0:T(8,128)(2,1)S(1)}, s32[32,128]{1,0:T(8,128)S(1)}) custom-call(s32[3,16]{1,0:T(4,128)S(1)} %get-tuple-element.39.refs_0_.near_list_ref, s32[3,16]{1,0:T(4,128)S(1)} %get-tuple-element.40.refs_1_.leaf_links_ref, ...), custom_call_target="tpu_custom_call" | custom-call | flops 100000000 | bytes 1048576 | tf_op jit(solution)/shard_map/interior_first/pallas_call | solution.py:517
  19.5 0.0 collective-permute-done.core_ref
  19.5 0.0 collective-permute-done.1.chip_ref
  19.5 1.2 %edges.2 = (f32[4,16,256]{2,1,0:T(8,128)S(1)}, f32[16,512]{1,0:T(8,128)S(1)}) custom-call(s32[3,16]{1,0:T(4,128)S(1)} %get-tuple-element.39.refs_0_.near_list_ref, s32[3,16]{1,0:T(4,128)S(1)} %get-tuple-element.40.refs_1_.leaf_links_ref, bf16[16,16,256]{2,1,0:T(8,128)(2,1)S(1)} %get-tuple-element.45.refs_2_.value_ref, ...), custom_call_target="tpu_custom_call" | custom-call | flops 1000000 | bytes 1048576 | tf_op jit(solution)/shard_map/edges/pallas_call | solution.py:528
  20.7 0.2 all-to-all-done.refs_3_
  20.8 2.8 %middle.1 = (f32[16,16,256]{2,1,0:T(8,128)S(1)}, bf16[16,16,256]{2,1,0:T(8,128)(2,1)S(1)}, bf16[16,32,64]{2,1,0:T(8,128)(2,1)S(1)}, bf16[32,24,128]{2,1,0:T(8,12...) custom-call(s32[1,3]{1,0:T(1,128)S(1)} %get-tuple-element.41.refs_0_, ...), custom_call_target="tpu_custom_call" | custom-call | flops 1000000 | bytes 1048576 | tf_op jit(solution)/shard_map/middle/pallas_call | solution.py:543
  23.7 4.6 %all-to-all-start.1 = ((bf16[32,24,128]{2,1,0:T(8,128)(2,1)}), bf16[32,24,128]{2,1,0:T(8,128)(2,1)S(1)}, u32[]{:S(2)}, u32[]{:S(2)}) async-start(bf16[32,24,128]{2,1,0:T(8,128)(2,1)} %get-tuple-element.68), calls=%async_computation.1 | async-start | bytes 393216 | tf_op jit(solution)/shard_map/all_to_all | solution.py:533
  28.2 0.3 collective-permute-start.2
  28.6 3.4 %collective-permute-start.3 = (bf16[128,128]{1,0:T(8,128)(2,1)S(1)}, bf16[128,128]{1,0:T(8,128)(2,1)S(1)}, u32[]{:S(2)}, u32[]{:S(2)}) collective-permute-start(bf16[128,128]{1,0:T(8,128)(2,1)S(1)} %get-tuple-element.72), channel_id=1, source_target_pairs={{1,2},{2,1},{3,4},{4,3},{5,6},{6,5},{7,8},{8,7},{9,10},{10,9},{11,... | collective-permute-start | bytes 98312 | tf_op jit(solution)/shard_map/ppermute | solution.py:435
  32.0 4.8 %interior_second.1 = (f32[12,16,256]{2,1,0:T(8,128)S(1)}, f32[16,512]{1,0:T(8,128)S(1)}, bf16[4,768,256]{2,1,0:T(8,128)(2,1)S(1)}, f32[16,4096]{1,0:T(8,128)}) custom-call(s32[3,16]{1,0:T(4,128)S(1)} %get-tuple-element.39.refs_0_.near_list_ref, s32[3,16]{1,0:T(4,128)S(1)} %get-tuple-element.40.refs_1_.leaf_links_ref, ...), custom_call_target="tpu_custom_call" | custom-call | flops 100000000 | bytes 1048576 | tf_op jit(solution)/shard_map/interior_second/pallas_call | solution.py:517
  36.8 0.0 collective-permute-done.2.core_ref
  36.8 0.0 collective-permute-done.3.chip_ref
  36.8 1.2 %edges.3 = (f32[4,16,256]{2,1,0:T(8,128)S(1)}, f32[16,512]{1,0:T(8,128)S(1)}) custom-call(s32[3,16]{1,0:T(4,128)S(1)} %get-tuple-element.39.refs_0_.near_list_ref, s32[3,16]{1,0:T(4,128)S(1)} %get-tuple-element.40.refs_1_.leaf_links_ref, bf16[16,16,256]{2,1,0:T(8,128)(2,1)S(1)} %get-tuple-element.63.refs_2_.value_ref, ...), custom_call_target="tpu_custom_call" | custom-call | flops 1000000 | bytes 1048576 | tf_op jit(solution)/shard_map/edges/pallas_call | solution.py:528
  38.0 0.0 all-to-all-done.1.refs_3_
  38.0 3.6 %end.1 = f32[16,4096]{1,0:T(8,128)} custom-call(s32[1,3]{1,0:T(1,128)S(1)} %get-tuple-element.41.refs_0_, s32[1,3]{1,0:T(1,128)S(1)} %get-tuple-element.42.refs_1_, s32[1,3]{1,0:T(1,128)S(1)} %get-tuple-element.43.refs_2_, bf16[32,24,128]{2,1,0:T(8,128)(2,1)S(1)} %all-to-all-done.1.refs_3_, f32[12,16,256]{2,1,0:T(8,128)S(1)} %get-tuple-element.69.refs_4_, ...), custom_call_target="tpu_custom_call" | custom-call | flops 1000000 | bytes 1048576 | tf_op jit(solution)/shard_map/end/pallas_call | solution.py:552
Async XLA Ops:
  4.5 16.3 %all-to-all-start = ((bf16[32,24,128]{2,1,0:T(8,128)(2,1)}), bf16[32,24,128]{2,1,0:T(8,128)(2,1)S(1)}, u32[]{:S(2)}, u32[]{:S(2)}) async-start(bf16[32,24,128]{2,1,0:T(8,128)(2,1)} %get-tuple-element.44), calls=%async_computation | async-start | bytes 393216 | tf_op jit(solution)/shard_map/all_to_all | solution.py:533
  11.6 7.8 %collective-permute-start = (bf16[128,128]{1,0:T(8,128)(2,1)S(1)}, bf16[128,128]{1,0:T(8,128)(2,1)S(1)}, u32[]{:S(2)}, u32[]{:S(2)}) collective-permute-start(bf16[128,128]{1,0:T(8,128)(2,1)S(1)} %get-tuple-element.51), channel_id=1, source_target_pairs={{0,1},{1,0},{2,3},{3,2},{4,5},{5,4},{6,7},{7,6},{8,9},{9,8},{10,11... | collective-permute-start | bytes 98312 | tf_op jit(solution)/shard_map/ppermute | solution.py:436
  12.0 7.5 %collective-permute-start.1 = (bf16[128,128]{1,0:T(8,128)(2,1)S(1)}, bf16[128,128]{1,0:T(8,128)(2,1)S(1)}, u32[]{:S(2)}, u32[]{:S(2)}) collective-permute-start(bf16[128,128]{1,0:T(8,128)(2,1)S(1)} %get-tuple-element.52), channel_id=1, source_target_pairs={{1,2},{2,1},{3,4},{4,3},{5,6},{6,5},{7,8},{8,7},{9,10},{10,9},{11,... | collective-permute-start | bytes 98312 | tf_op jit(solution)/shard_map/ppermute | solution.py:435
  23.7 14.3 %all-to-all-start.1 = ((bf16[32,24,128]{2,1,0:T(8,128)(2,1)}), bf16[32,24,128]{2,1,0:T(8,128)(2,1)S(1)}, u32[]{:S(2)}, u32[]{:S(2)}) async-start(bf16[32,24,128]{2,1,0:T(8,128)(2,1)} %get-tuple-element.68), calls=%async_computation.1 | async-start | bytes 393216 | tf_op jit(solution)/shard_map/all_to_all | solution.py:533
  28.2 8.5 %collective-permute-start.2 = (bf16[128,128]{1,0:T(8,128)(2,1)S(1)}, bf16[128,128]{1,0:T(8,128)(2,1)S(1)}, u32[]{:S(2)}, u32[]{:S(2)}) collective-permute-start(bf16[128,128]{1,0:T(8,128)(2,1)S(1)} %get-tuple-element.71), channel_id=1, source_target_pairs={{0,1},{1,0},{2,3},{3,2},{4,5},{5,4},{6,7},{7,6},{8,9},{9,8},{10,11... | collective-permute-start | bytes 98312 | tf_op jit(solution)/shard_map/ppermute | solution.py:436
  28.6 8.2 %collective-permute-start.3 = (bf16[128,128]{1,0:T(8,128)(2,1)S(1)}, bf16[128,128]{1,0:T(8,128)(2,1)S(1)}, u32[]{:S(2)}, u32[]{:S(2)}) collective-permute-start(bf16[128,128]{1,0:T(8,128)(2,1)S(1)} %get-tuple-element.72), channel_id=1, source_target_pairs={{1,2},{2,1},{3,4},{4,3},{5,6},{6,5},{7,8},{8,7},{9,10},{10,9},{11,... | collective-permute-start | bytes 98312 | tf_op jit(solution)/shard_map/ppermute | solution.py:435

commit v3 on v2

--- a/solution.py
+++ b/solution.py
@@ -272,12 +272,14 @@
 
 
 def near_product(value_ref, near_list_ref, tiles_ref, l, slot, shift):
-    sources = [value_ref[near_list_ref[k, l] + shift] for k in range(near_list_ref.shape[0])]
+    near_list = near_list_ref[...]
+    sources = [value_ref[near_list[k, l] + shift] for k in range(near_list.shape[0])]
     return dot(jnp.concatenate(sources, axis=1), tiles_ref[slot])
 
 
 def leaf_coupling(moment_ref, leaf_links_ref, coupling_ref, l, shift):
-    picked = [moment_ref[leaf_links_ref[k, l] + shift] for k in range(leaf_links_ref.shape[0])]
+    leaf_links = leaf_links_ref[...]
+    picked = [moment_ref[leaf_links[k, l] + shift] for k in range(leaf_links.shape[0])]
     return coupled_halves(picked, coupling_ref[l])
 
 
@@ -323,13 +325,16 @@
     def block_moment(c):
         return sum(term_ref[c * gz + j, :rhs_count, rank:].astype(F32) for j in range(gz))
 
-    link_count = device_links_ref.shape[1]
-    top_field = coupled([top_moment(top_links_ref[0, k]) for k in range(link_count)], top_coupling_ref[0])
+    device_links, block_links, top_links = (
+        device_links_ref[...], block_links_ref[...], top_links_ref[...]
+    )
+    link_count = device_links.shape[1]
+    top_field = coupled([top_moment(top_links[0, k]) for k in range(link_count)], top_coupling_ref[0])
     block_field = coupled(
-        [block_moment(block_links_ref[0, k]) for k in range(link_count)], block_coupling_ref[0]
+        [block_moment(block_links[0, k]) for k in range(link_count)], block_coupling_ref[0]
     ) + dot_nt(top_field, block_transfer_ref[0])
     device_field = coupled(
-        [term_ref[device_links_ref[0, k], :rhs_count, :rank] for k in range(link_count)],
+        [term_ref[device_links[0, k], :rhs_count, :rank] for k in range(link_count)],
         device_coupling_ref[0],
     ) + dot_nt(block_field, device_transfer_ref[0])
     edge = LINK_REACH * rank
@@ -378,7 +383,7 @@
 
     writes = []
     end = 0
-    for columns in permuted(read, inverse_ref, table_ref, (True, True, False), rhs_count):
+    for columns in permuted(read, inverse_ref, table_ref, (True, True, True, False), rhs_count):
         start, end = end, end + columns.shape[1]
         out_buf[:, start:end] = columns
         if end % part == 0:
@@ -401,7 +406,6 @@
 
 
 VMEM = pl.BlockSpec(memory_space=pltpu.VMEM)
-SMEM = pl.BlockSpec(memory_space=pltpu.SMEM)
 HBM = pl.BlockSpec(memory_space=pltpu.HBM)
 MIB = 1 << 20
 CHUNK = 4
@@ -479,7 +483,7 @@
         "start",
         [HBM] * (1 + len(kept + lists)),
         outs,
-        out_specs=(VMEM,) * (5 + len(kept)) + (SMEM,) * len(lists),
+        out_specs=(VMEM,) * (5 + len(kept + lists)),
         scratch=[
             pltpu.VMEM((rhs_count, point_count), F32),
             pltpu.SemaphoreType.DMA((1 + len(kept + lists),)),
@@ -517,7 +521,7 @@
         return call(
             functools.partial(interior_kernel, second),
             "interior_second" if second else "interior_first",
-            [SMEM] * 2 + [VMEM] * 3 + [HBM] + [VMEM] * len(more),
+            [VMEM] * 5 + [HBM] + [VMEM] * len(more),
             inside_outs + (last_out,),
             out_specs=(VMEM,) * 3 + (out_spec,),
             scratch=scratch,
@@ -525,7 +529,7 @@
         )(near_list, leaf_links, value, moment, coupling, in_hbm(near_tiles), *more)
 
     def edges(tiles):
-        return call(edge_kernel, "edges", [SMEM] * 2 + [VMEM] * 6, edge_outs, scratch=edge_scratch)(
+        return call(edge_kernel, "edges", [VMEM] * 8, edge_outs, scratch=edge_scratch)(
             near_list, leaf_links, value, moment, core, chip, coupling, tiles
         )
 
@@ -541,7 +545,7 @@
     near, field, tiles, inverse_order = interior(False, inverse_out, VMEM, tile_scratch, order)
     edge_near, edge_field = edges(tiles)
     first, value, moment, term, core, chip = call(
-        middle_kernel, "middle", [SMEM] * 3 + [VMEM] * 12, (wide_out, value_out) + up_outs,
+        middle_kernel, "middle", [VMEM] * 15, (wide_out, value_out) + up_outs,
     )(*coarse_links, term, near, field, edge_near, edge_field, *coarse)
     core, chip = exchange(core, chip)
     term = spread(term)
@@ -550,7 +554,7 @@
     )
     edge_near, edge_field = edges(tiles)
     twice = call(
-        end_kernel, "end", [SMEM] * 3 + [VMEM] * 13, points_out, out_specs=HBM,
+        end_kernel, "end", [VMEM] * 16, points_out, out_specs=HBM,
         scratch=[pltpu.VMEM(wide_out.shape, F32)] + out_scratch,
     )(*coarse_links, term, near, field, edge_near, edge_field, *coarse, inverse_order)
     return smoothed, twice

time: 41.9 us -> 39.4 us (0.940)
  Pallas kernels: 21.6 us -> 18.5 us
  waiting for transfers between devices: 0.2 us -> 1.59 us
  starting transfers between devices: 19.1 us -> 18.3 us
    pallas_call x4, Pallas kernels: 8.82 us -> 6.62 us  [the longest x1 2.96 us: shards(): call(end_kernel, 'end', [VMEM] * 16, points_out, out_specs=HBM, scratch=[...]
    all_to_all x2, waiting for transfers between devices: 0.19 us -> 1.58 us  [spread(): return lax.all_to_all(term, AXES, 0, 0)]
    pallas_call x2, Pallas kernels: 8.9 us -> 8.03 us  [interior(): call(functools.partial(interior_kernel, second), 'interior_second' if sec...]
    all_to_all x2, starting transfers between devices: 11.7 us -> 10.9 us  [spread(): return lax.all_to_all(term, AXES, 0, 0)]
  transfers between devices with their start and end apart: 6 -> 6, of which waited for: 1 -> 2; matrix products, arithmetic and copies ran while one was open for 0% -> 0% of each run, Pallas kernels for 27% -> 24%
where the time goes in v3:
time: 39.4 us; the launch traced here: 39.2 us
  Pallas kernels  18.5 us (47%)
  starting transfers between devices  18.3 us (46%)
  waiting for transfers between devices  1.59 us (4%)
  between operations  0.73 us (2%)
    all_to_all x2, starting transfers between devices, spread(): return lax.all_to_all(term, AXES, 0, 0)  10.9 us
    pallas_call x2, Pallas kernels, interior(): call(functools.partial(interior_kernel, second), 'interior_second' if sec...  8.03 us
    ppermute x2, starting transfers between devices, exchange(): chip = lax.ppermute(chip, AXES, outer)  6.77 us
    pallas_call x1, Pallas kernels, shards(): call(start_kernel, 'start', [HBM] * (1 + len(kept + lists)), outs, out_sp...  3.84 us
    pallas_call x1, Pallas kernels, shards(): call(end_kernel, 'end', [VMEM] * 16, points_out, out_specs=HBM, scratch=[...  2.96 us
    pallas_call x1, Pallas kernels, shards(): call(middle_kernel, 'middle', [VMEM] * 15, (wide_out, value_out) + up_outs)  2.36 us
    all_to_all x2, waiting for transfers between devices, spread(): return lax.all_to_all(term, AXES, 0, 0)  1.58 us
    pallas_call x2, Pallas kernels, edges(): call(edge_kernel, 'edges', [VMEM] * 8, edge_outs, scratch=edge_scratch)  1.3 us
  transfers between devices with their start and end apart: 6, of which 2 were waited for; matrix products, arithmetic and copies ran while one was open for 0% of the time, Pallas kernels for 24%

profile of v3, /device:TPU:1, one launch (start us, length us, event | category | flops | bytes accessed | tf_op | source)
XLA Modules:
  0.0 39.2 jit_solution(17203100921640005538)
XLA Ops:
  0.6 3.8 %start.1 = (bf16[16,16,256]{2,1,0:T(8,128)(2,1)S(1)}, bf16[16,32,64]{2,1,0:T(8,128)(2,1)S(1)}, bf16[32,24,128]{2,1,0:T(8,128)(2,1)}, bf16[128,128]{1,0:T(8,128)(...) custom-call(f32[16,4096]{1,0:T(8,128)} %refs_0_.1, ...), custom_call_target="tpu_custom_call" | custom-call | flops 1000000 | bytes 1048576 | tf_op jit(solution)/shard_map/start/pallas_call | solution.py:481
  4.5 7.1 %all-to-all-start = ((bf16[32,24,128]{2,1,0:T(8,128)(2,1)}), bf16[32,24,128]{2,1,0:T(8,128)(2,1)S(1)}, u32[]{:S(2)}, u32[]{:S(2)}) async-start(bf16[32,24,128]{2,1,0:T(8,128)(2,1)} %get-tuple-element.44), calls=%async_computation | async-start | bytes 393216 | tf_op jit(solution)/shard_map/all_to_all | solution.py:537
  11.6 0.3 collective-permute-start
  11.9 3.4 %collective-permute-start.1 = (bf16[128,128]{1,0:T(8,128)(2,1)S(1)}, bf16[128,128]{1,0:T(8,128)(2,1)S(1)}, u32[]{:S(2)}, u32[]{:S(2)}) collective-permute-start(bf16[128,128]{1,0:T(8,128)(2,1)S(1)} %get-tuple-element.52), channel_id=1, source_target_pairs={{1,2},{2,1},{3,4},{4,3},{5,6},{6,5},{7,8},{8,7},{9,10},{10,9},{11,... | collective-permute-start | bytes 98312 | tf_op jit(solution)/shard_map/ppermute | solution.py:439
  15.3 3.9 %interior_first.1 = (f32[12,16,256]{2,1,0:T(8,128)S(1)}, f32[16,512]{1,0:T(8,128)S(1)}, bf16[4,768,256]{2,1,0:T(8,128)(2,1)S(1)}, s32[32,128]{1,0:T(8,128)S(1)}) custom-call(s32[3,16]{1,0:T(4,128)S(1)} %get-tuple-element.39.refs_0_.near_list_ref, s32[3,16]{1,0:T(4,128)S(1)} %get-tuple-element.40.refs_1_.leaf_links_ref, ...), custom_call_target="tpu_custom_call" | custom-call | flops 100000000 | bytes 1048576 | tf_op jit(solution)/shard_map/interior_first/pallas_call | solution.py:521
  19.2 0.0 collective-permute-done.core_ref
  19.2 0.0 collective-permute-done.1.chip_ref
  19.2 0.7 %edges.2 = (f32[4,16,256]{2,1,0:T(8,128)S(1)}, f32[16,512]{1,0:T(8,128)S(1)}) custom-call(s32[3,16]{1,0:T(4,128)S(1)} %get-tuple-element.39.refs_0_.near_list_ref, s32[3,16]{1,0:T(4,128)S(1)} %get-tuple-element.40.refs_1_.leaf_links_ref, bf16[16,16,256]{2,1,0:T(8,128)(2,1)S(1)} %get-tuple-element.45.refs_2_.value_ref, ...), custom_call_target="tpu_custom_call" | custom-call | flops 1000000 | bytes 1048576 | tf_op jit(solution)/shard_map/edges/pallas_call | solution.py:532
  19.9 0.9 %all-to-all-done.refs_3_ = bf16[32,24,128]{2,1,0:T(8,128)(2,1)S(1)} async-done(((bf16[32,24,128]{2,1,0:T(8,128)(2,1)}), bf16[32,24,128]{2,1,0:T(8,128)(2,1)S(1)}, u32[]{:S(2)}, u32[]{:S(2)}) %all-to-all-start) | async-done | bytes 196640 | tf_op jit(solution)/shard_map/all_to_all | solution.py:537
  20.8 2.4 %middle.1 = (f32[16,16,256]{2,1,0:T(8,128)S(1)}, bf16[16,16,256]{2,1,0:T(8,128)(2,1)S(1)}, bf16[16,32,64]{2,1,0:T(8,128)(2,1)S(1)}, bf16[32,24,128]{2,1,0:T(8,12...) custom-call(s32[1,3]{1,0:T(1,128)S(1)} %get-tuple-element.41.refs_0_, ...), custom_call_target="tpu_custom_call" | custom-call | flops 1000000 | bytes 1048576 | tf_op jit(solution)/shard_map/middle/pallas_call | solution.py:547
  23.2 3.8 %all-to-all-start.1 = ((bf16[32,24,128]{2,1,0:T(8,128)(2,1)}), bf16[32,24,128]{2,1,0:T(8,128)(2,1)S(1)}, u32[]{:S(2)}, u32[]{:S(2)}) async-start(bf16[32,24,128]{2,1,0:T(8,128)(2,1)} %get-tuple-element.68), calls=%async_computation.1 | async-start | bytes 393216 | tf_op jit(solution)/shard_map/all_to_all | solution.py:537
  27.0 0.3 collective-permute-start.2
  27.3 3.4 %collective-permute-start.3 = (bf16[128,128]{1,0:T(8,128)(2,1)S(1)}, bf16[128,128]{1,0:T(8,128)(2,1)S(1)}, u32[]{:S(2)}, u32[]{:S(2)}) collective-permute-start(bf16[128,128]{1,0:T(8,128)(2,1)S(1)} %get-tuple-element.72), channel_id=1, source_target_pairs={{1,2},{2,1},{3,4},{4,3},{5,6},{6,5},{7,8},{8,7},{9,10},{10,9},{11,... | collective-permute-start | bytes 98312 | tf_op jit(solution)/shard_map/ppermute | solution.py:439
  30.7 4.1 %interior_second.1 = (f32[12,16,256]{2,1,0:T(8,128)S(1)}, f32[16,512]{1,0:T(8,128)S(1)}, bf16[4,768,256]{2,1,0:T(8,128)(2,1)S(1)}, f32[16,4096]{1,0:T(8,128)}) custom-call(s32[3,16]{1,0:T(4,128)S(1)} %get-tuple-element.39.refs_0_.near_list_ref, s32[3,16]{1,0:T(4,128)S(1)} %get-tuple-element.40.refs_1_.leaf_links_ref, ...), custom_call_target="tpu_custom_call" | custom-call | flops 100000000 | bytes 1048576 | tf_op jit(solution)/shard_map/interior_second/pallas_call | solution.py:521
  34.9 0.0 collective-permute-done.2.core_ref
  34.9 0.0 collective-permute-done.3.chip_ref
  34.9 0.7 %edges.3 = (f32[4,16,256]{2,1,0:T(8,128)S(1)}, f32[16,512]{1,0:T(8,128)S(1)}) custom-call(s32[3,16]{1,0:T(4,128)S(1)} %get-tuple-element.39.refs_0_.near_list_ref, s32[3,16]{1,0:T(4,128)S(1)} %get-tuple-element.40.refs_1_.leaf_links_ref, bf16[16,16,256]{2,1,0:T(8,128)(2,1)S(1)} %get-tuple-element.63.refs_2_.value_ref, ...), custom_call_target="tpu_custom_call" | custom-call | flops 1000000 | bytes 1048576 | tf_op jit(solution)/shard_map/edges/pallas_call | solution.py:532
  35.5 0.7 %all-to-all-done.1.refs_3_ = bf16[32,24,128]{2,1,0:T(8,128)(2,1)S(1)} async-done(((bf16[32,24,128]{2,1,0:T(8,128)(2,1)}), bf16[32,24,128]{2,1,0:T(8,128)(2,1)S(1)}, u32[]{:S(2)}, u32[]{:S(2)}) %all-to-all-start.1) | async-done | bytes 196640 | tf_op jit(solution)/shard_map/all_to_all | solution.py:537
  36.2 3.0 %end.1 = f32[16,4096]{1,0:T(8,128)} custom-call(s32[1,3]{1,0:T(1,128)S(1)} %get-tuple-element.41.refs_0_, s32[1,3]{1,0:T(1,128)S(1)} %get-tuple-element.42.refs_1_, s32[1,3]{1,0:T(1,128)S(1)} %get-tuple-element.43.refs_2_, bf16[32,24,128]{2,1,0:T(8,128)(2,1)S(1)} %all-to-all-done.1.refs_3_, f32[12,16,256]{2,1,0:T(8,128)S(1)} %get-tuple-element.69.refs_4_, ...), custom_call_target="tpu_custom_call" | custom-call | flops 1000000 | bytes 1048576 | tf_op jit(solution)/shard_map/end/pallas_call | solution.py:556
Async XLA Ops:
  4.5 16.3 %all-to-all-start = ((bf16[32,24,128]{2,1,0:T(8,128)(2,1)}), bf16[32,24,128]{2,1,0:T(8,128)(2,1)S(1)}, u32[]{:S(2)}, u32[]{:S(2)}) async-start(bf16[32,24,128]{2,1,0:T(8,128)(2,1)} %get-tuple-element.44), calls=%async_computation | async-start | bytes 393216 | tf_op jit(solution)/shard_map/all_to_all | solution.py:537
  11.6 7.6 %collective-permute-start = (bf16[128,128]{1,0:T(8,128)(2,1)S(1)}, bf16[128,128]{1,0:T(8,128)(2,1)S(1)}, u32[]{:S(2)}, u32[]{:S(2)}) collective-permute-start(bf16[128,128]{1,0:T(8,128)(2,1)S(1)} %get-tuple-element.51), channel_id=1, source_target_pairs={{0,1},{1,0},{2,3},{3,2},{4,5},{5,4},{6,7},{7,6},{8,9},{9,8},{10,11... | collective-permute-start | bytes 98312 | tf_op jit(solution)/shard_map/ppermute | solution.py:440
  11.9 7.3 %collective-permute-start.1 = (bf16[128,128]{1,0:T(8,128)(2,1)S(1)}, bf16[128,128]{1,0:T(8,128)(2,1)S(1)}, u32[]{:S(2)}, u32[]{:S(2)}) collective-permute-start(bf16[128,128]{1,0:T(8,128)(2,1)S(1)} %get-tuple-element.52), channel_id=1, source_target_pairs={{1,2},{2,1},{3,4},{4,3},{5,6},{6,5},{7,8},{8,7},{9,10},{10,9},{11,... | collective-permute-start | bytes 98312 | tf_op jit(solution)/shard_map/ppermute | solution.py:439
  23.2 13.0 %all-to-all-start.1 = ((bf16[32,24,128]{2,1,0:T(8,128)(2,1)}), bf16[32,24,128]{2,1,0:T(8,128)(2,1)S(1)}, u32[]{:S(2)}, u32[]{:S(2)}) async-start(bf16[32,24,128]{2,1,0:T(8,128)(2,1)} %get-tuple-element.68), calls=%async_computation.1 | async-start | bytes 393216 | tf_op jit(solution)/shard_map/all_to_all | solution.py:537
  27.0 7.9 %collective-permute-start.2 = (bf16[128,128]{1,0:T(8,128)(2,1)S(1)}, bf16[128,128]{1,0:T(8,128)(2,1)S(1)}, u32[]{:S(2)}, u32[]{:S(2)}) collective-permute-start(bf16[128,128]{1,0:T(8,128)(2,1)S(1)} %get-tuple-element.71), channel_id=1, source_target_pairs={{0,1},{1,0},{2,3},{3,2},{4,5},{5,4},{6,7},{7,6},{8,9},{9,8},{10,11... | collective-permute-start | bytes 98312 | tf_op jit(solution)/shard_map/ppermute | solution.py:440
  27.3 7.6 %collective-permute-start.3 = (bf16[128,128]{1,0:T(8,128)(2,1)S(1)}, bf16[128,128]{1,0:T(8,128)(2,1)S(1)}, u32[]{:S(2)}, u32[]{:S(2)}) collective-permute-start(bf16[128,128]{1,0:T(8,128)(2,1)S(1)} %get-tuple-element.72), channel_id=1, source_target_pairs={{1,2},{2,1},{3,4},{4,3},{5,6},{6,5},{7,8},{8,7},{9,10},{10,9},{11,... | collective-permute-start | bytes 98312 | tf_op jit(solution)/shard_map/ppermute | solution.py:439

commit v4 on v3

--- a/solution.py
+++ b/solution.py
@@ -144,11 +144,11 @@
 
 
 def start_kernel(*refs):
-    signal_buf, sems = refs[-2:]
-    kept_count = (len(refs) - 2 - 1 - 5) // 2
+    signal_buf, table_ref, sems = refs[-3:]
+    kept_count = (len(refs) - 3 - 1 - 5) // 2
     sources = refs[: 1 + kept_count]
     value_ref, *outs = refs[1 + kept_count : 6 + kept_count]
-    kept = refs[6 + kept_count : -2]
+    kept = refs[6 + kept_count : -3]
     order_ref, basis_ref, transfer_ref, device_transfer_ref, block_transfer_ref = kept[:5]
     rhs_count, point_count = signal_buf.shape
     tiles = point_count // LANES
@@ -165,13 +165,14 @@
 
     for copy in copies[:2]:
         copy.wait()
+    for t in range(tiles):
+        columns = signal_buf[:, t * LANES : (t + 1) * LANES]
+        table_ref[t * rhs_count : (t + 1) * rhs_count] = columns.astype(BF16)
+    parts = list(permuted(read, order_ref, table_ref, (True, False), rhs_count))
+    per_leaf = len(parts) // leaf_count
     values = []
     for l in range(leaf_count):
-        parts = [
-            moved_lanes(read, order_ref[t : t + 1, :], tiles, rhs_count)
-            for t in range(l * leaf // LANES, (l + 1) * leaf // LANES)
-        ]
-        value = jnp.concatenate(parts, axis=1).astype(BF16)
+        value = jnp.concatenate(parts[l * per_leaf : (l + 1) * per_leaf], axis=1).astype(BF16)
         value_ref[l] = value
         values.append(value)
     for copy in copies[2:6]:
@@ -486,6 +487,7 @@
         out_specs=(VMEM,) * (5 + len(kept + lists)),
         scratch=[
             pltpu.VMEM((rhs_count, point_count), F32),
+            pltpu.VMEM((column_tiles * rhs_count, LANES), BF16),
             pltpu.SemaphoreType.DMA((1 + len(kept + lists),)),
         ],
     )(*map(in_hbm, (signal, *kept, *lists)))

time: 39.4 us -> 39.2 us (level)
  no operation moved by 1% of the time
where the time goes in v4:
time: 39.2 us; the launch traced here: 38.9 us
  starting transfers between devices  18.3 us (47%)
  Pallas kernels  18.2 us (46%)
  waiting for transfers between devices  1.59 us (4%)
  between operations  0.73 us (2%)
    all_to_all x2, starting transfers between devices, spread(): return lax.all_to_all(term, AXES, 0, 0)  10.9 us
    pallas_call x2, Pallas kernels, interior(): call(functools.partial(interior_kernel, second), 'interior_second' if sec...  8.03 us
    ppermute x2, starting transfers between devices, exchange(): chip = lax.ppermute(chip, AXES, outer)  6.77 us
    pallas_call x1, Pallas kernels, shards(): call(start_kernel, 'start', [HBM] * (1 + len(kept + lists)), outs, out_sp...  3.56 us
    pallas_call x1, Pallas kernels, shards(): call(end_kernel, 'end', [VMEM] * 16, points_out, out_specs=HBM, scratch=[...  2.96 us
    pallas_call x1, Pallas kernels, shards(): call(middle_kernel, 'middle', [VMEM] * 15, (wide_out, value_out) + up_outs)  2.36 us
    all_to_all x2, waiting for transfers between devices, spread(): return lax.all_to_all(term, AXES, 0, 0)  1.58 us
    pallas_call x2, Pallas kernels, edges(): call(edge_kernel, 'edges', [VMEM] * 8, edge_outs, scratch=edge_scratch)  1.3 us
  transfers between devices with their start and end apart: 6, of which 2 were waited for; matrix products, arithmetic and copies ran while one was open for 0% of the time, Pallas kernels for 24%

profile of v4, /device:TPU:1, one launch (start us, length us, event | category | flops | bytes accessed | tf_op | source)
XLA Modules:
  0.0 38.9 jit_solution(461231353913742598)
XLA Ops:
  0.6 3.6 %start.1 = (bf16[16,16,256]{2,1,0:T(8,128)(2,1)S(1)}, bf16[16,32,64]{2,1,0:T(8,128)(2,1)S(1)}, bf16[32,24,128]{2,1,0:T(8,128)(2,1)}, bf16[128,128]{1,0:T(8,128)(...) custom-call(f32[16,4096]{1,0:T(8,128)} %refs_0_.1, ...), custom_call_target="tpu_custom_call" | custom-call | flops 1000000 | bytes 1048576 | tf_op jit(solution)/shard_map/start/pallas_call | solution.py:482
  4.2 7.1 %all-to-all-start = ((bf16[32,24,128]{2,1,0:T(8,128)(2,1)}), bf16[32,24,128]{2,1,0:T(8,128)(2,1)S(1)}, u32[]{:S(2)}, u32[]{:S(2)}) async-start(bf16[32,24,128]{2,1,0:T(8,128)(2,1)} %get-tuple-element.44), calls=%async_computation | async-start | bytes 393216 | tf_op jit(solution)/shard_map/all_to_all | solution.py:539
  11.3 0.3 collective-permute-start
  11.6 3.4 %collective-permute-start.1 = (bf16[128,128]{1,0:T(8,128)(2,1)S(1)}, bf16[128,128]{1,0:T(8,128)(2,1)S(1)}, u32[]{:S(2)}, u32[]{:S(2)}) collective-permute-start(bf16[128,128]{1,0:T(8,128)(2,1)S(1)} %get-tuple-element.52), channel_id=1, source_target_pairs={{1,2},{2,1},{3,4},{4,3},{5,6},{6,5},{7,8},{8,7},{9,10},{10,9},{11,... | collective-permute-start | bytes 98312 | tf_op jit(solution)/shard_map/ppermute | solution.py:440
  15.0 3.9 %interior_first.1 = (f32[12,16,256]{2,1,0:T(8,128)S(1)}, f32[16,512]{1,0:T(8,128)S(1)}, bf16[4,768,256]{2,1,0:T(8,128)(2,1)S(1)}, s32[32,128]{1,0:T(8,128)S(1)}) custom-call(s32[3,16]{1,0:T(4,128)S(1)} %get-tuple-element.39.refs_0_.near_list_ref, s32[3,16]{1,0:T(4,128)S(1)} %get-tuple-element.40.refs_1_.leaf_links_ref, ...), custom_call_target="tpu_custom_call" | custom-call | flops 100000000 | bytes 1048576 | tf_op jit(solution)/shard_map/interior_first/pallas_call | solution.py:523
  18.9 0.0 collective-permute-done.core_ref
  18.9 0.0 collective-permute-done.1.chip_ref
  18.9 0.7 %edges.2 = (f32[4,16,256]{2,1,0:T(8,128)S(1)}, f32[16,512]{1,0:T(8,128)S(1)}) custom-call(s32[3,16]{1,0:T(4,128)S(1)} %get-tuple-element.39.refs_0_.near_list_ref, s32[3,16]{1,0:T(4,128)S(1)} %get-tuple-element.40.refs_1_.leaf_links_ref, bf16[16,16,256]{2,1,0:T(8,128)(2,1)S(1)} %get-tuple-element.45.refs_2_.value_ref, ...), custom_call_target="tpu_custom_call" | custom-call | flops 1000000 | bytes 1048576 | tf_op jit(solution)/shard_map/edges/pallas_call | solution.py:534
  19.6 0.9 %all-to-all-done.refs_3_ = bf16[32,24,128]{2,1,0:T(8,128)(2,1)S(1)} async-done(((bf16[32,24,128]{2,1,0:T(8,128)(2,1)}), bf16[32,24,128]{2,1,0:T(8,128)(2,1)S(1)}, u32[]{:S(2)}, u32[]{:S(2)}) %all-to-all-start) | async-done | bytes 196640 | tf_op jit(solution)/shard_map/all_to_all | solution.py:539
  20.5 2.4 %middle.1 = (f32[16,16,256]{2,1,0:T(8,128)S(1)}, bf16[16,16,256]{2,1,0:T(8,128)(2,1)S(1)}, bf16[16,32,64]{2,1,0:T(8,128)(2,1)S(1)}, bf16[32,24,128]{2,1,0:T(8,12...) custom-call(s32[1,3]{1,0:T(1,128)S(1)} %get-tuple-element.41.refs_0_, ...), custom_call_target="tpu_custom_call" | custom-call | flops 1000000 | bytes 1048576 | tf_op jit(solution)/shard_map/middle/pallas_call | solution.py:549
  22.9 3.8 %all-to-all-start.1 = ((bf16[32,24,128]{2,1,0:T(8,128)(2,1)}), bf16[32,24,128]{2,1,0:T(8,128)(2,1)S(1)}, u32[]{:S(2)}, u32[]{:S(2)}) async-start(bf16[32,24,128]{2,1,0:T(8,128)(2,1)} %get-tuple-element.68), calls=%async_computation.1 | async-start | bytes 393216 | tf_op jit(solution)/shard_map/all_to_all | solution.py:539
  26.7 0.3 collective-permute-start.2
  27.0 3.4 %collective-permute-start.3 = (bf16[128,128]{1,0:T(8,128)(2,1)S(1)}, bf16[128,128]{1,0:T(8,128)(2,1)S(1)}, u32[]{:S(2)}, u32[]{:S(2)}) collective-permute-start(bf16[128,128]{1,0:T(8,128)(2,1)S(1)} %get-tuple-element.72), channel_id=1, source_target_pairs={{1,2},{2,1},{3,4},{4,3},{5,6},{6,5},{7,8},{8,7},{9,10},{10,9},{11,... | collective-permute-start | bytes 98312 | tf_op jit(solution)/shard_map/ppermute | solution.py:440
  30.4 4.1 %interior_second.1 = (f32[12,16,256]{2,1,0:T(8,128)S(1)}, f32[16,512]{1,0:T(8,128)S(1)}, bf16[4,768,256]{2,1,0:T(8,128)(2,1)S(1)}, f32[16,4096]{1,0:T(8,128)}) custom-call(s32[3,16]{1,0:T(4,128)S(1)} %get-tuple-element.39.refs_0_.near_list_ref, s32[3,16]{1,0:T(4,128)S(1)} %get-tuple-element.40.refs_1_.leaf_links_ref, ...), custom_call_target="tpu_custom_call" | custom-call | flops 100000000 | bytes 1048576 | tf_op jit(solution)/shard_map/interior_second/pallas_call | solution.py:523
  34.6 0.0 collective-permute-done.2.core_ref
  34.6 0.0 collective-permute-done.3.chip_ref
  34.6 0.7 %edges.3 = (f32[4,16,256]{2,1,0:T(8,128)S(1)}, f32[16,512]{1,0:T(8,128)S(1)}) custom-call(s32[3,16]{1,0:T(4,128)S(1)} %get-tuple-element.39.refs_0_.near_list_ref, s32[3,16]{1,0:T(4,128)S(1)} %get-tuple-element.40.refs_1_.leaf_links_ref, bf16[16,16,256]{2,1,0:T(8,128)(2,1)S(1)} %get-tuple-element.63.refs_2_.value_ref, ...), custom_call_target="tpu_custom_call" | custom-call | flops 1000000 | bytes 1048576 | tf_op jit(solution)/shard_map/edges/pallas_call | solution.py:534
  35.2 0.7 %all-to-all-done.1.refs_3_ = bf16[32,24,128]{2,1,0:T(8,128)(2,1)S(1)} async-done(((bf16[32,24,128]{2,1,0:T(8,128)(2,1)}), bf16[32,24,128]{2,1,0:T(8,128)(2,1)S(1)}, u32[]{:S(2)}, u32[]{:S(2)}) %all-to-all-start.1) | async-done | bytes 196640 | tf_op jit(solution)/shard_map/all_to_all | solution.py:539
  35.9 3.0 %end.1 = f32[16,4096]{1,0:T(8,128)} custom-call(s32[1,3]{1,0:T(1,128)S(1)} %get-tuple-element.41.refs_0_, s32[1,3]{1,0:T(1,128)S(1)} %get-tuple-element.42.refs_1_, s32[1,3]{1,0:T(1,128)S(1)} %get-tuple-element.43.refs_2_, bf16[32,24,128]{2,1,0:T(8,128)(2,1)S(1)} %all-to-all-done.1.refs_3_, f32[12,16,256]{2,1,0:T(8,128)S(1)} %get-tuple-element.69.refs_4_, ...), custom_call_target="tpu_custom_call" | custom-call | flops 1000000 | bytes 1048576 | tf_op jit(solution)/shard_map/end/pallas_call | solution.py:558
Async XLA Ops:
  4.2 16.3 %all-to-all-start = ((bf16[32,24,128]{2,1,0:T(8,128)(2,1)}), bf16[32,24,128]{2,1,0:T(8,128)(2,1)S(1)}, u32[]{:S(2)}, u32[]{:S(2)}) async-start(bf16[32,24,128]{2,1,0:T(8,128)(2,1)} %get-tuple-element.44), calls=%async_computation | async-start | bytes 393216 | tf_op jit(solution)/shard_map/all_to_all | solution.py:539
  11.3 7.6 %collective-permute-start = (bf16[128,128]{1,0:T(8,128)(2,1)S(1)}, bf16[128,128]{1,0:T(8,128)(2,1)S(1)}, u32[]{:S(2)}, u32[]{:S(2)}) collective-permute-start(bf16[128,128]{1,0:T(8,128)(2,1)S(1)} %get-tuple-element.51), channel_id=1, source_target_pairs={{0,1},{1,0},{2,3},{3,2},{4,5},{5,4},{6,7},{7,6},{8,9},{9,8},{10,11... | collective-permute-start | bytes 98312 | tf_op jit(solution)/shard_map/ppermute | solution.py:441
  11.6 7.3 %collective-permute-start.1 = (bf16[128,128]{1,0:T(8,128)(2,1)S(1)}, bf16[128,128]{1,0:T(8,128)(2,1)S(1)}, u32[]{:S(2)}, u32[]{:S(2)}) collective-permute-start(bf16[128,128]{1,0:T(8,128)(2,1)S(1)} %get-tuple-element.52), channel_id=1, source_target_pairs={{1,2},{2,1},{3,4},{4,3},{5,6},{6,5},{7,8},{8,7},{9,10},{10,9},{11,... | collective-permute-start | bytes 98312 | tf_op jit(solution)/shard_map/ppermute | solution.py:440
  22.9 13.0 %all-to-all-start.1 = ((bf16[32,24,128]{2,1,0:T(8,128)(2,1)}), bf16[32,24,128]{2,1,0:T(8,128)(2,1)S(1)}, u32[]{:S(2)}, u32[]{:S(2)}) async-start(bf16[32,24,128]{2,1,0:T(8,128)(2,1)} %get-tuple-element.68), calls=%async_computation.1 | async-start | bytes 393216 | tf_op jit(solution)/shard_map/all_to_all | solution.py:539
  26.7 7.9 %collective-permute-start.2 = (bf16[128,128]{1,0:T(8,128)(2,1)S(1)}, bf16[128,128]{1,0:T(8,128)(2,1)S(1)}, u32[]{:S(2)}, u32[]{:S(2)}) collective-permute-start(bf16[128,128]{1,0:T(8,128)(2,1)S(1)} %get-tuple-element.71), channel_id=1, source_target_pairs={{0,1},{1,0},{2,3},{3,2},{4,5},{5,4},{6,7},{7,6},{8,9},{9,8},{10,11... | collective-permute-start | bytes 98312 | tf_op jit(solution)/shard_map/ppermute | solution.py:441
  27.0 7.6 %collective-permute-start.3 = (bf16[128,128]{1,0:T(8,128)(2,1)S(1)}, bf16[128,128]{1,0:T(8,128)(2,1)S(1)}, u32[]{:S(2)}, u32[]{:S(2)}) collective-permute-start(bf16[128,128]{1,0:T(8,128)(2,1)S(1)} %get-tuple-element.72), channel_id=1, source_target_pairs={{1,2},{2,1},{3,4},{4,3},{5,6},{6,5},{7,8},{8,7},{9,10},{10,9},{11,... | collective-permute-start | bytes 98312 | tf_op jit(solution)/shard_map/ppermute | solution.py:440
